TPU v7x, 256 devices: a whole 4x4x8 slice. The times are simulated.
256 devices in a mesh: row: 4 (over y), sa: 4 (over x), ha: 16 (over z, core).
Axes of the slice: x: 4, y: 4, z: 8, core: 2. Of those that a mesh axis runs over, the one named last changes fastest.
Arguments:
- records: float32 [64, 16, 65536], P(None, 'sa', ('row', 'ha')), parts along dimension 2, may hold values from -6 to 6
- halo_mass: float32 [16, 65536], P('sa', ('row', 'ha')), parts along dimension 1, may hold values from 0.1 to 10
- forest_id: int32 [16, 65536], P('sa', ('row', 'ha')), parts along dimension 1, may hold values from 0 to 8191, as said below
- dest_block: int32 [16, 65536], P('sa', ('row', 'ha')), parts along dimension 1, may hold values from 0 to 2559, as said below
- dest_slot: int32 [16, 65536], P('sa', ('row', 'ha')), parts along dimension 1, may hold values from 0 to 127
Outputs:
- blocks: float32 [64, 10240, 128], P(None, ('row', 'sa', 'ha')), parts along dimension 1
- block_mass: float32 [10240, 128], P(('row', 'sa', 'ha')), parts along dimension 0
- forest_mass: float32 [32768], P(('row', 'sa', 'ha')), parts along dimension 0
- forest_mean: float32 [64, 32768], P(None, ('row', 'sa', 'ha')), parts along dimension 1
- forest_second: float32 [64, 32768], P(None, ('row', 'sa', 'ha')), parts along dimension 1
There are 4 independent parts, one for each index of `row`. A program takes and returns all parts, laid end to end along the dimension named above; each array names one. Nothing has to cross between parts.
Inputs may be any that keep to these rules, and one draw needn't show every extreme that they name: The pairs (dest_block, dest_slot) are distinct over all halos. Block b lies on the device of index b // 40 of sa+ha (sa slowest), and forest f is owned by the device of index f // 128; every halo goes to a block of its forest's owner. On each device the used slots are the first ones in block-then-slot order, and every forest has at least one halo. `forest_id`: of the halos of one device (one index of sa and one of ha), at most 88 go to blocks of one device; in every draw some pair of devices reaches 88, and some device has all its 5120 slots used.
All inputs are finite; a program needn't handle non-finite values.
Results may differ from a plain program's by a relative error of at most 0.0003.
Values sent between devices are 32-bit elements; how exact they have to be, the bound alone decides.
No kernel may reach another device: no remote copies, remote signals or barrier semaphores. Data moves between devices by JAX's collectives and lax.ppermute only.
A program may use at most 64 MiB of HBM per device.

v0:
```python
import jax
import jax.numpy as jnp
from jax import lax
from jax.sharding import Mesh
from jax.sharding import PartitionSpec as P

FOR_DEV = 128
BLK_DEV = 40
HA = ("ha_0", "ha_1")
SA_HA = ("sa", "ha_0", "ha_1")
ROW_HA = ("row", "ha_0", "ha_1")
ROW_SA_HA = ("row", "sa", "ha_0", "ha_1")


def in_one_piece(arrays, axis, split_dim, concat_dim, along):
    widths = [a.shape[along] for a in arrays]
    both = jnp.concatenate(arrays, axis=along)
    result = lax.all_to_all(both, axis, split_axis=split_dim, concat_axis=concat_dim, tiled=True)
    return tuple(jnp.split(result, [sum(widths[:k]) for k in range(1, len(widths))], axis=along))


def by_axis(array, axes):
    for axis in axes:
        array = lax.psum(array, axis)
    return array


def tiled_place(source, target, width, tile_cols):
    tile_count = (width + tile_cols - 1) // tile_cols

    def one_tile(tile_index):
        columns = tile_index * tile_cols + jnp.arange(tile_cols, dtype=jnp.int32)
        select = (target[:, None] == columns[None, :]).astype(jnp.float32)
        return jnp.dot(
            source, select, precision=lax.Precision.HIGHEST, preferred_element_type=jnp.float32
        )

    pieces = lax.map(one_tile, jnp.arange(tile_count, dtype=jnp.int32))
    placed = jnp.moveaxis(pieces, 0, 1).reshape(source.shape[0], tile_count * tile_cols)
    return placed


def bucket_ranks(owner_dev, peer_count):
    local_count = owner_dev.shape[0]
    span = 512
    group_count = local_count // span
    member = (
        owner_dev.reshape(group_count, span)[:, :, None]
        == jnp.arange(peer_count, dtype=jnp.int32)[None, None, :]
    ).astype(jnp.bfloat16)
    lower = (jnp.arange(span)[:, None] > jnp.arange(span)[None, :]).astype(jnp.bfloat16)
    within = jnp.einsum("ij,bjp->bip", lower, member, preferred_element_type=jnp.float32)
    totals = jnp.sum(member.astype(jnp.float32), axis=1)
    earlier = (jnp.arange(group_count)[:, None] > jnp.arange(group_count)[None, :]).astype(
        jnp.float32
    )
    before = jnp.dot(
        earlier, totals, precision=lax.Precision.HIGHEST, preferred_element_type=jnp.float32
    )
    counted = (within + before[:, None, :]) * member.astype(jnp.float32)
    return jnp.sum(counted, axis=2).reshape(local_count).astype(jnp.int32)


def on_device(records, halo_mass, forest_id, dest_block, dest_slot):
    sa_count = lax.axis_size("sa")
    ha_count = lax.axis_size(HA)
    peer_count = sa_count * ha_count
    fields = records.shape[0]
    local_count = records.shape[1] * records.shape[2]
    capacity = 11 * (local_count // peer_count) // 8
    slots_dev = BLK_DEV * 128
    width_out = peer_count * capacity
    flat = records.reshape(fields, local_count)
    weights_in = halo_mass.reshape(local_count)
    block_in = dest_block.reshape(local_count)
    forest_in = forest_id.reshape(local_count)
    owner_dev = block_in // BLK_DEV
    target = owner_dev * capacity + bucket_ranks(owner_dev, peer_count)
    slot_local = block_in % BLK_DEV * 128 + dest_slot.reshape(local_count)
    source = jnp.concatenate(
        [
            flat,
            weights_in[None, :],
            (slot_local + 1).astype(jnp.float32)[None, :],
            (forest_in % FOR_DEV + 1).astype(jnp.float32)[None, :],
        ]
    )
    packed = tiled_place(source, target, width_out, min(512, width_out))
    outbox = packed[:fields]
    labels = packed[fields:]
    arrived = in_one_piece(
        (outbox.reshape(fields, peer_count, capacity), labels.reshape(3, peer_count, capacity)),
        SA_HA,
        1,
        1,
        0,
    )
    incoming = arrived[0].reshape(fields, width_out)
    tags = arrived[1].reshape(3, width_out)
    slot_tag = tags[1].astype(jnp.int32) - 1
    arranged = tiled_place(
        jnp.concatenate([incoming, tags[0:1], tags[2:3]]), slot_tag, slots_dev, 512
    )
    blocks = arranged[:fields]
    slot_mass = arranged[fields]
    slot_forest = arranged[fields + 1].astype(jnp.int32) - 1
    member = (slot_forest[None, :] == jnp.arange(FOR_DEV, dtype=jnp.int32)[:, None]).astype(
        jnp.float32
    )
    scaled = slot_mass[None, :] * blocks
    weighted = jnp.concatenate([slot_mass[None, :], scaled, scaled * blocks])
    owned = lax.dot_general(
        weighted,
        member,
        (((1,), (1,)), ((), ())),
        precision=lax.Precision.HIGHEST,
        preferred_element_type=jnp.float32,
    )
    mass_sum = by_axis(jnp.sum(weights_in), SA_HA)
    weight = owned[0]
    forest_mass = weight * (FOR_DEV * peer_count / mass_sum)
    forest_mean = owned[1 : 1 + fields] / weight[None, :]
    forest_second = owned[1 + fields :] / weight[None, :]
    return (
        blocks.reshape(fields, BLK_DEV, 128),
        slot_mass.reshape(BLK_DEV, 128),
        forest_mass,
        forest_mean,
        forest_second,
    )


def solution(mesh):
    split = Mesh(
        mesh.devices.reshape(mesh.shape["row"], mesh.shape["sa"], 8, 2),
        ("row", "sa", "ha_0", "ha_1"),
    )
    in_specs = (
        P(None, "sa", ROW_HA),
        P("sa", ROW_HA),
        P("sa", ROW_HA),
        P("sa", ROW_HA),
        P("sa", ROW_HA),
    )
    out_specs = (
        P(None, ROW_SA_HA, None),
        P(ROW_SA_HA, None),
        P(ROW_SA_HA),
        P(None, ROW_SA_HA),
        P(None, ROW_SA_HA),
    )
    return jax.shard_map(
        on_device, mesh=split, in_specs=in_specs, out_specs=out_specs, check_vma=False
    )
```

profile of v0, /device:TPU:1, one launch (start us, length us, event | category | flops | bytes accessed | tf_op | source)
XLA Modules:
  0.0 213.5 jit_solution(12950665837986819936)
XLA Ops:
  0.6 0.8 fusion.51
  1.5 0.7 fusion.45
  2.2 0.7 remainder_bitcast_fusion
  3.0 0.7 copy.34
  3.7 0.7 copy.33
  4.5 0.7 copy.31
  6.2 0.6 copy.30
  7.0 47.6 %while.20 = (s32[]{:T(128)}, f32[11,67,512]{2,1,0:T(8,128)S(1)}, s32[4096]{0:T(1024)S(1)}, s32[11]{0:T(128)S(1)}, f32[67,4096]{1,0:T(8,128)S(1)}, /*index=5*/s32[]{:T(128)}, s32[1]{0:T(128)}) while((s32[]{:T(128)}, f32[11,67,512]{2,1,0:T(8,128)S(1)}, s32[4096]{0:T(1024)S(1)}, s32[11]{0:T(128)S(1)}, f32[67,4096]{1,0:T(8,128)S(1)}, ...), condition=%wide.region_3.4_spmd, body=%wide.region_2.3_spmd.sunk | while | flops 1688207872 | bytes 1347701 | solution.py:38
  7.0 0.6 dynamic_slice.10
  8.3 3.1 %fusion.60 = f32[11,67,512]{2,1,0:T(8,128)S(1)} fusion(f32[11,67,512]{2,1,0:T(8,128)S(1)} %get-tuple-element.163, s32[]{:T(128)S(6)} %copy.41, f32[67,4096]{1,0:T(8,128)S(1)} %get-tuple-element.173, s32[512]{0:T(512)S(1)} %iota_add_fusion.4, s32[4096]{0:T(1024)S(1)} %get-tuple-element.171), kind=kOutput, calls=%fused_computation.5.clone.1 | convolution fusion | flops 1688207360 | bytes 1345540 | tf_op jit(solution)/shard_map/while/body/eval_jaxpr/dot_general | solution.py:34
  12.6 3.1 %fusion.60 = f32[11,67,512]{2,1,0:T(8,128)S(1)} fusion(f32[11,67,512]{2,1,0:T(8,128)S(1)} %get-tuple-element.163, s32[]{:T(128)S(6)} %copy.41, f32[67,4096]{1,0:T(8,128)S(1)} %get-tuple-element.173, s32[512]{0:T(512)S(1)} %iota_add_fusion.4, s32[4096]{0:T(1024)S(1)} %get-tuple-element.171), kind=kOutput, calls=%fused_computation.5.clone.1 | convolution fusion | flops 1688207360 | bytes 1345540 | tf_op jit(solution)/shard_map/while/body/eval_jaxpr/dot_general | solution.py:34
  16.9 3.1 %fusion.60 = f32[11,67,512]{2,1,0:T(8,128)S(1)} fusion(f32[11,67,512]{2,1,0:T(8,128)S(1)} %get-tuple-element.163, s32[]{:T(128)S(6)} %copy.41, f32[67,4096]{1,0:T(8,128)S(1)} %get-tuple-element.173, s32[512]{0:T(512)S(1)} %iota_add_fusion.4, s32[4096]{0:T(1024)S(1)} %get-tuple-element.171), kind=kOutput, calls=%fused_computation.5.clone.1 | convolution fusion | flops 1688207360 | bytes 1345540 | tf_op jit(solution)/shard_map/while/body/eval_jaxpr/dot_general | solution.py:34
  21.3 3.1 %fusion.60 = f32[11,67,512]{2,1,0:T(8,128)S(1)} fusion(f32[11,67,512]{2,1,0:T(8,128)S(1)} %get-tuple-element.163, s32[]{:T(128)S(6)} %copy.41, f32[67,4096]{1,0:T(8,128)S(1)} %get-tuple-element.173, s32[512]{0:T(512)S(1)} %iota_add_fusion.4, s32[4096]{0:T(1024)S(1)} %get-tuple-element.171), kind=kOutput, calls=%fused_computation.5.clone.1 | convolution fusion | flops 1688207360 | bytes 1345540 | tf_op jit(solution)/shard_map/while/body/eval_jaxpr/dot_general | solution.py:34
  25.6 3.1 %fusion.60 = f32[11,67,512]{2,1,0:T(8,128)S(1)} fusion(f32[11,67,512]{2,1,0:T(8,128)S(1)} %get-tuple-element.163, s32[]{:T(128)S(6)} %copy.41, f32[67,4096]{1,0:T(8,128)S(1)} %get-tuple-element.173, s32[512]{0:T(512)S(1)} %iota_add_fusion.4, s32[4096]{0:T(1024)S(1)} %get-tuple-element.171), kind=kOutput, calls=%fused_computation.5.clone.1 | convolution fusion | flops 1688207360 | bytes 1345540 | tf_op jit(solution)/shard_map/while/body/eval_jaxpr/dot_general | solution.py:34
  29.9 3.1 %fusion.60 = f32[11,67,512]{2,1,0:T(8,128)S(1)} fusion(f32[11,67,512]{2,1,0:T(8,128)S(1)} %get-tuple-element.163, s32[]{:T(128)S(6)} %copy.41, f32[67,4096]{1,0:T(8,128)S(1)} %get-tuple-element.173, s32[512]{0:T(512)S(1)} %iota_add_fusion.4, s32[4096]{0:T(1024)S(1)} %get-tuple-element.171), kind=kOutput, calls=%fused_computation.5.clone.1 | convolution fusion | flops 1688207360 | bytes 1345540 | tf_op jit(solution)/shard_map/while/body/eval_jaxpr/dot_general | solution.py:34
  34.2 3.1 %fusion.60 = f32[11,67,512]{2,1,0:T(8,128)S(1)} fusion(f32[11,67,512]{2,1,0:T(8,128)S(1)} %get-tuple-element.163, s32[]{:T(128)S(6)} %copy.41, f32[67,4096]{1,0:T(8,128)S(1)} %get-tuple-element.173, s32[512]{0:T(512)S(1)} %iota_add_fusion.4, s32[4096]{0:T(1024)S(1)} %get-tuple-element.171), kind=kOutput, calls=%fused_computation.5.clone.1 | convolution fusion | flops 1688207360 | bytes 1345540 | tf_op jit(solution)/shard_map/while/body/eval_jaxpr/dot_general | solution.py:34
  38.5 3.1 %fusion.60 = f32[11,67,512]{2,1,0:T(8,128)S(1)} fusion(f32[11,67,512]{2,1,0:T(8,128)S(1)} %get-tuple-element.163, s32[]{:T(128)S(6)} %copy.41, f32[67,4096]{1,0:T(8,128)S(1)} %get-tuple-element.173, s32[512]{0:T(512)S(1)} %iota_add_fusion.4, s32[4096]{0:T(1024)S(1)} %get-tuple-element.171), kind=kOutput, calls=%fused_computation.5.clone.1 | convolution fusion | flops 1688207360 | bytes 1345540 | tf_op jit(solution)/shard_map/while/body/eval_jaxpr/dot_general | solution.py:34
  42.9 3.1 %fusion.60 = f32[11,67,512]{2,1,0:T(8,128)S(1)} fusion(f32[11,67,512]{2,1,0:T(8,128)S(1)} %get-tuple-element.163, s32[]{:T(128)S(6)} %copy.41, f32[67,4096]{1,0:T(8,128)S(1)} %get-tuple-element.173, s32[512]{0:T(512)S(1)} %iota_add_fusion.4, s32[4096]{0:T(1024)S(1)} %get-tuple-element.171), kind=kOutput, calls=%fused_computation.5.clone.1 | convolution fusion | flops 1688207360 | bytes 1345540 | tf_op jit(solution)/shard_map/while/body/eval_jaxpr/dot_general | solution.py:34
  47.2 3.1 %fusion.60 = f32[11,67,512]{2,1,0:T(8,128)S(1)} fusion(f32[11,67,512]{2,1,0:T(8,128)S(1)} %get-tuple-element.163, s32[]{:T(128)S(6)} %copy.41, f32[67,4096]{1,0:T(8,128)S(1)} %get-tuple-element.173, s32[512]{0:T(512)S(1)} %iota_add_fusion.4, s32[4096]{0:T(1024)S(1)} %get-tuple-element.171), kind=kOutput, calls=%fused_computation.5.clone.1 | convolution fusion | flops 1688207360 | bytes 1345540 | tf_op jit(solution)/shard_map/while/body/eval_jaxpr/dot_general | solution.py:34
  51.5 3.1 %fusion.60 = f32[11,67,512]{2,1,0:T(8,128)S(1)} fusion(f32[11,67,512]{2,1,0:T(8,128)S(1)} %get-tuple-element.163, s32[]{:T(128)S(6)} %copy.41, f32[67,4096]{1,0:T(8,128)S(1)} %get-tuple-element.173, s32[512]{0:T(512)S(1)} %iota_add_fusion.4, s32[4096]{0:T(1024)S(1)} %get-tuple-element.171), kind=kOutput, calls=%fused_computation.5.clone.1 | convolution fusion | flops 1688207360 | bytes 1345540 | tf_op jit(solution)/shard_map/while/body/eval_jaxpr/dot_general | solution.py:34
  54.8 0.8 reshape.226
  55.5 0.9 copy.20
  56.4 3.3 %reshape.225 = f32[64,64,88]{2,1,0:T(8,128)} reshape(f32[64,11,512]{2,1,0:T(8,128)S(1)} %copy.20) | data formatting | bytes 2883584 | tf_op jit(solution)/shard_map/reshape | solution.py:92
  59.7 1.8 pad_maximum_fusion
  61.5 2.7 %copy.22 = f32[67,64,88]{2,0,1:T(8,128)} copy(f32[67,64,88]{2,1,0:T(8,128)S(1)} %pad_maximum_fusion) | data formatting | bytes 3018752 | tf_op jit(solution)/shard_map/concatenate | solution.py:17
  64.1 13.1 %all-to-all-start = ((f32[67,64,88]{2,0,1:T(8,128)}), f32[67,64,88]{2,0,1:T(8,128)S(1)}, u32[]{:S(2)}, u32[]{:S(2)}) async-start(f32[67,64,88]{2,0,1:T(8,128)} %copy.22), calls=%async_computation | async-start | bytes 4718592 | tf_op jit(solution)/shard_map/all_to_all | solution.py:18
  77.3 0.6 reduce_sum.29
  77.9 10.2 %psum.21 = f32[]{:T(128)} all-reduce(f32[]{:T(128)} %reduce_sum.29), channel_id=1, replica_groups=mesh['row'=4,'sa'=4,'ha_0'=8,'ha_1'=2] {'sa'}, use_global_device_ids=true, to_apply=%region_7.8 | all-reduce | flops 1 | bytes 8 | tf_op jit(solution)/shard_map/psum | solution.py:24
  88.0 50.5 %psum.22 = f32[]{:T(128)} all-reduce(f32[]{:T(128)} %psum.21), channel_id=1, replica_groups=mesh['row'=4,'sa'=4,'ha_0'=8,'ha_1'=2] {'ha_0'}, use_global_device_ids=true, to_apply=%region_8.9 | all-reduce | flops 1 | bytes 8 | tf_op jit(solution)/shard_map/psum | solution.py:24
  138.5 6.0 %psum.23 = f32[]{:T(128)} all-reduce(f32[]{:T(128)} %psum.22), channel_id=1, replica_groups=mesh['row'=4,'sa'=4,'ha_0'=8,'ha_1'=2] {'ha_1'}, use_global_device_ids=true, to_apply=%region_9.10 | all-reduce | flops 1 | bytes 8 | tf_op jit(solution)/shard_map/psum | solution.py:24
  145.7 2.5 %copy.23 = f32[64,64,88]{2,1,0:T(8,128)} copy(f32[64,64,88]{2,0,1:T(8,128)S(1)} %split.5) | data formatting | bytes 2883584 | tf_op jit(solution)/shard_map/split | solution.py:19
  148.3 3.3 %reshape.227 = f32[64,5632]{1,0:T(8,128)} reshape(f32[64,64,88]{2,1,0:T(8,128)} %copy.23) | data formatting | bytes 2883584 | tf_op jit(solution)/shard_map/reshape | solution.py:98
  152.0 1.6 pad_maximum_fusion.1
  153.7 54.0 %while.21 = (s32[]{:T(128)}, f32[10,66,512]{2,1,0:T(8,128)S(1)}, s32[5632]{0:T(1024)S(1)}, s32[10]{0:T(128)S(1)}, f32[66,5632]{1,0:T(8,128)S(1)}, /*index=5*/s32[]{:T(128)}, s32[1]{0:T(128)}) while((s32[]{:T(128)}, f32[10,66,512]{2,1,0:T(8,128)S(1)}, s32[5632]{0:T(1024)S(1)}, s32[10]{0:T(128)S(1)}, f32[66,5632]{1,0:T(8,128)S(1)}, ...), condition=%wide.region_5.6_spmd, body=%wide.region_4.5_spmd.sunk | while | flops 2286682624 | bytes 1798261 | solution.py:38
  154.9 4.1 %fusion.63 = f32[10,66,512]{2,1,0:T(8,128)S(1)} fusion(f32[10,66,512]{2,1,0:T(8,128)S(1)} %get-tuple-element.184, s32[]{:T(128)S(6)} %copy.47, f32[66,5632]{1,0:T(8,128)S(1)} %get-tuple-element.194, s32[512]{0:T(512)S(1)} %iota_add_fusion.5, s32[5632]{0:T(1024)S(1)} %get-tuple-element.192), kind=kOutput, calls=%fused_computation.12.clone.1 | convolution fusion | flops 2286682112 | bytes 1796100 | tf_op jit(solution)/shard_map/while/body/eval_jaxpr/dot_general | solution.py:34
  160.3 4.1 %fusion.63 = f32[10,66,512]{2,1,0:T(8,128)S(1)} fusion(f32[10,66,512]{2,1,0:T(8,128)S(1)} %get-tuple-element.184, s32[]{:T(128)S(6)} %copy.47, f32[66,5632]{1,0:T(8,128)S(1)} %get-tuple-element.194, s32[512]{0:T(512)S(1)} %iota_add_fusion.5, s32[5632]{0:T(1024)S(1)} %get-tuple-element.192), kind=kOutput, calls=%fused_computation.12.clone.1 | convolution fusion | flops 2286682112 | bytes 1796100 | tf_op jit(solution)/shard_map/while/body/eval_jaxpr/dot_general | solution.py:34
  165.7 4.1 %fusion.63 = f32[10,66,512]{2,1,0:T(8,128)S(1)} fusion(f32[10,66,512]{2,1,0:T(8,128)S(1)} %get-tuple-element.184, s32[]{:T(128)S(6)} %copy.47, f32[66,5632]{1,0:T(8,128)S(1)} %get-tuple-element.194, s32[512]{0:T(512)S(1)} %iota_add_fusion.5, s32[5632]{0:T(1024)S(1)} %get-tuple-element.192), kind=kOutput, calls=%fused_computation.12.clone.1 | convolution fusion | flops 2286682112 | bytes 1796100 | tf_op jit(solution)/shard_map/while/body/eval_jaxpr/dot_general | solution.py:34
  171.1 4.1 %fusion.63 = f32[10,66,512]{2,1,0:T(8,128)S(1)} fusion(f32[10,66,512]{2,1,0:T(8,128)S(1)} %get-tuple-element.184, s32[]{:T(128)S(6)} %copy.47, f32[66,5632]{1,0:T(8,128)S(1)} %get-tuple-element.194, s32[512]{0:T(512)S(1)} %iota_add_fusion.5, s32[5632]{0:T(1024)S(1)} %get-tuple-element.192), kind=kOutput, calls=%fused_computation.12.clone.1 | convolution fusion | flops 2286682112 | bytes 1796100 | tf_op jit(solution)/shard_map/while/body/eval_jaxpr/dot_general | solution.py:34
  176.5 4.1 %fusion.63 = f32[10,66,512]{2,1,0:T(8,128)S(1)} fusion(f32[10,66,512]{2,1,0:T(8,128)S(1)} %get-tuple-element.184, s32[]{:T(128)S(6)} %copy.47, f32[66,5632]{1,0:T(8,128)S(1)} %get-tuple-element.194, s32[512]{0:T(512)S(1)} %iota_add_fusion.5, s32[5632]{0:T(1024)S(1)} %get-tuple-element.192), kind=kOutput, calls=%fused_computation.12.clone.1 | convolution fusion | flops 2286682112 | bytes 1796100 | tf_op jit(solution)/shard_map/while/body/eval_jaxpr/dot_general | solution.py:34
  181.9 4.1 %fusion.63 = f32[10,66,512]{2,1,0:T(8,128)S(1)} fusion(f32[10,66,512]{2,1,0:T(8,128)S(1)} %get-tuple-element.184, s32[]{:T(128)S(6)} %copy.47, f32[66,5632]{1,0:T(8,128)S(1)} %get-tuple-element.194, s32[512]{0:T(512)S(1)} %iota_add_fusion.5, s32[5632]{0:T(1024)S(1)} %get-tuple-element.192), kind=kOutput, calls=%fused_computation.12.clone.1 | convolution fusion | flops 2286682112 | bytes 1796100 | tf_op jit(solution)/shard_map/while/body/eval_jaxpr/dot_general | solution.py:34
  187.3 4.1 %fusion.63 = f32[10,66,512]{2,1,0:T(8,128)S(1)} fusion(f32[10,66,512]{2,1,0:T(8,128)S(1)} %get-tuple-element.184, s32[]{:T(128)S(6)} %copy.47, f32[66,5632]{1,0:T(8,128)S(1)} %get-tuple-element.194, s32[512]{0:T(512)S(1)} %iota_add_fusion.5, s32[5632]{0:T(1024)S(1)} %get-tuple-element.192), kind=kOutput, calls=%fused_computation.12.clone.1 | convolution fusion | flops 2286682112 | bytes 1796100 | tf_op jit(solution)/shard_map/while/body/eval_jaxpr/dot_general | solution.py:34
  192.7 4.1 %fusion.63 = f32[10,66,512]{2,1,0:T(8,128)S(1)} fusion(f32[10,66,512]{2,1,0:T(8,128)S(1)} %get-tuple-element.184, s32[]{:T(128)S(6)} %copy.47, f32[66,5632]{1,0:T(8,128)S(1)} %get-tuple-element.194, s32[512]{0:T(512)S(1)} %iota_add_fusion.5, s32[5632]{0:T(1024)S(1)} %get-tuple-element.192), kind=kOutput, calls=%fused_computation.12.clone.1 | convolution fusion | flops 2286682112 | bytes 1796100 | tf_op jit(solution)/shard_map/while/body/eval_jaxpr/dot_general | solution.py:34
  198.1 4.1 %fusion.63 = f32[10,66,512]{2,1,0:T(8,128)S(1)} fusion(f32[10,66,512]{2,1,0:T(8,128)S(1)} %get-tuple-element.184, s32[]{:T(128)S(6)} %copy.47, f32[66,5632]{1,0:T(8,128)S(1)} %get-tuple-element.194, s32[512]{0:T(512)S(1)} %iota_add_fusion.5, s32[5632]{0:T(1024)S(1)} %get-tuple-element.192), kind=kOutput, calls=%fused_computation.12.clone.1 | convolution fusion | flops 2286682112 | bytes 1796100 | tf_op jit(solution)/shard_map/while/body/eval_jaxpr/dot_general | solution.py:34
  203.5 4.1 %fusion.63 = f32[10,66,512]{2,1,0:T(8,128)S(1)} fusion(f32[10,66,512]{2,1,0:T(8,128)S(1)} %get-tuple-element.184, s32[]{:T(128)S(6)} %copy.47, f32[66,5632]{1,0:T(8,128)S(1)} %get-tuple-element.194, s32[512]{0:T(512)S(1)} %iota_add_fusion.5, s32[5632]{0:T(1024)S(1)} %get-tuple-element.192), kind=kOutput, calls=%fused_computation.12.clone.1 | convolution fusion | flops 2286682112 | bytes 1796100 | tf_op jit(solution)/shard_map/while/body/eval_jaxpr/dot_general | solution.py:34
  208.3 2.0 fusion.20
  210.8 0.6 slice_divide_fusion
  211.4 0.8 copy.24
  212.2 1.2 reshape.228
  (84 shorter events, 15.1 us)
Async XLA Ops:
  0.6 5.5 %copy-start.1 = (f32[64,4,1024]{2,1,0:T(4,128)S(1)}, f32[64,4,1024]{2,1,0:T(4,128)}, u32[]{:S(2)}) copy-start(f32[64,4,1024]{2,1,0:T(4,128)} %param.9) | copy-start | bytes 3145732
  56.4 3.3 %copy-start.2 = (f32[3,64,88]{2,1,0:T(8,128)S(1)}, f32[3,64,88]{2,1,0:T(8,128)}, u32[]{:S(2)}) copy-start(f32[3,64,88]{2,1,0:T(8,128)} %reshape.226) | copy-start | bytes 202756
  64.1 13.1 %copy-start.4 = (f32[4,1024]{1,0:T(4,128)S(1)}, f32[4,1024]{1,0:T(4,128)}, u32[]{:S(2)}) copy-start(f32[4,1024]{1,0:T(4,128)} %param.10) | copy-start | bytes 49156
  64.1 81.1 %all-to-all-start = ((f32[67,64,88]{2,0,1:T(8,128)}), f32[67,64,88]{2,0,1:T(8,128)S(1)}, u32[]{:S(2)}, u32[]{:S(2)}) async-start(f32[67,64,88]{2,0,1:T(8,128)} %copy.22), calls=%async_computation | async-start | bytes 4718592 | tf_op jit(solution)/shard_map/all_to_all | solution.py:18
  151.8 1.8 copy-start
  207.7 0.6 copy-start.3
where the time goes:
time: 214 us; the launch traced here: 213 us
  matrix products  77.7 us (36%)
  blocking collectives  66.7 us (31%)
  local copies, waits for them, and re-layouts  31.9 us (15%)
  loops' own time  14.1 us (7%)
  starting transfers between devices  13.1 us (6%)
  other arithmetic  8.31 us (4%)
    dot_general x21, matrix products, one_tile(): jnp.dot(source, select, precision=lax.Precision.HIGHEST, preferred_elemen...  75 us
    psum x3, blocking collectives, by_axis(): array = lax.psum(array, axis)  66.7 us
    another operation x2, loops' own time, tiled_place(): pieces = lax.map(one_tile, jnp.arange(tile_count, dtype=jnp.int32))  14.1 us
    all_to_all x1, starting transfers between devices, in_one_piece(): lax.all_to_all(both, axis, split_axis=split_dim, concat_axis=concat_dim,...  13.1 us
    dynamic_slice x21, local copies, waits for them, and re-layouts, tiled_place(): pieces = lax.map(one_tile, jnp.arange(tile_count, dtype=jnp.int32))  12.3 us
  transfers between devices with their start and end apart: 1, of which 0 were waited for; matrix products, arithmetic and copies ran while one was open for 0% of the time, Pallas kernels for 0%

commit v1 on v0

v1 whole, which is shorter than its diff:
```python
import functools

import jax
import jax.numpy as jnp
from jax import lax
from jax.experimental import pallas as pl
from jax.experimental.pallas import tpu as pltpu
from jax.sharding import Mesh
from jax.sharding import PartitionSpec as P

FIELDS = 64
FOR_DEV = 128
BLK_DEV = 40
SLOTS = BLK_DEV * 128
PEERS = 64
CAP = 88
ROWS = 48
SA_HA = ("sa", "ha_0", "ha_1")
ROW_HA = ("row", "ha_0", "ha_1")
ROW_SA_HA = ("row", "sa", "ha_0", "ha_1")


def iota(shape, dim):
    return lax.broadcasted_iota(jnp.int32, shape, dim)


def owner_of(block):
    return lax.shift_right_logical(block * 1639, 16)


def pack_kernel(rec, mass, forest, block, slot, out, placed, tile_a, tile_b, target_v, target_s, sem):
    snaps, halos = mass.shape
    per_snap = halos // 128
    before = (iota((256, 384), 0) < iota((256, 384), 1)) | (iota((256, 384), 1) >= 256)
    before = before.astype(jnp.float32).astype(jnp.bfloat16)
    peer = iota((PEERS, 256), 0)
    base = jnp.zeros((PEERS, 128), jnp.float32)
    for s in range(snaps):
        for q in range(halos // 256):
            own = owner_of(block[s : s + 1, 256 * q : 256 * q + 256])
            member = peer == own
            counts = jnp.dot(
                member.astype(jnp.float32).astype(jnp.bfloat16), before, preferred_element_type=jnp.float32
            )
            rank = counts[:, :256] + jnp.concatenate([base, base], axis=1)
            rank = jnp.sum(jnp.where(member, rank, 0.0), axis=0, keepdims=True)
            base = base + counts[:, 256:]
            target = own * CAP + rank.astype(jnp.int32)
            row = s * per_snap + 2 * q
            target_v[row : row + 1, :] = target[:, :128]
            target_v[row + 1 : row + 2, :] = target[:, 128:]
    copy = pltpu.make_async_copy(target_v, target_s, sem)
    copy.start()

    def clear(k, carry):
        placed[pl.ds(pl.multiple_of(k * 64, 64), 64), :] = jnp.zeros((64, 128), jnp.float32)
        return carry

    lax.fori_loop(0, PEERS * CAP // 64, clear, 0)
    copy.wait()
    first = iota((8, 128), 0) == 0
    none8 = jnp.zeros((8, 128), jnp.float32)

    def turn(s, group, tile):
        cols = pl.ds(pl.multiple_of(group * 128, 128), 128)
        blk = block[s : s + 1, cols]
        local = (blk - owner_of(blk) * BLK_DEV) * 128 + slot[s : s + 1, cols] + 1
        here = forest[s : s + 1, cols] & (FOR_DEV - 1)

        def label(row):
            return jnp.where(first, jnp.broadcast_to(row, (8, 128)), 0.0)

        stack = jnp.concatenate(
            [
                rec[:, s, cols],
                label(mass[s : s + 1, cols]),
                none8,
                label(local.astype(jnp.float32)),
                none8,
                label(here.astype(jnp.float32)),
                none8,
                none8,
                none8,
            ],
            axis=0,
        )
        tile[...] = stack.T

    def spread(group, tile):
        for i in range(128):
            placed[pl.ds(target_s[group, i], 1), :] = tile[i : i + 1, :]

    turn(0, 0, tile_a)
    for s in range(snaps):

        def step(k, carry):
            turn(s, 2 * k + 1, tile_b)
            spread(s * per_snap + 2 * k, tile_a)
            turn(s, 2 * k + 2, tile_a)
            spread(s * per_snap + 2 * k + 1, tile_b)
            return carry

        lax.fori_loop(0, per_snap // 2 - 1, step, 0)
        turn(s, per_snap - 1, tile_b)
        spread(s * per_snap + per_snap - 2, tile_a)
        if s + 1 < snaps:
            turn(s + 1, 0, tile_a)
        spread(s * per_snap + per_snap - 1, tile_b)

    lane = iota((8, 128), 1)
    low = lane < FIELDS
    total = jnp.sum(jnp.sum(mass[...], axis=0, keepdims=True), axis=1, keepdims=True)

    def squeeze(p, carry):
        start = p * CAP
        tiles = [placed[pl.ds(pl.multiple_of(start + 8 * v, 8), 8), :] for v in range(CAP // 8)]
        labels = jnp.where(lane == 127, jnp.broadcast_to(total, (8, 128)), 0.0)
        for v in range(CAP // 8):
            own = jnp.where(low, 0.0, tiles[v])
            labels = labels + (pltpu.roll(own, v, 1) if v else own)
        for v in range(5):
            out[p, 8 * v : 8 * v + 8, :] = jnp.where(low, tiles[v], pltpu.roll(tiles[v + 6], 64, 1))
        out[p, 40:48, :] = jnp.where(low, tiles[5], labels)
        return carry

    lax.fori_loop(0, PEERS, squeeze, 0)


def place_kernel(
    msg, blocks, block_mass, fmass, fmean, fsecond, placed, tile_a, tile_b, slot_v, slot_s, sem
):
    lane = iota((8, 128), 1)
    low = lane < FIELDS
    slot_lane = (lane >= 80) & (lane < 80 + CAP // 8)
    total = jnp.zeros((8, 128), jnp.float32)
    for g in range(PEERS // 8):
        acc = jnp.zeros((8, 128), jnp.float32)
        for k in range(8):
            labels = msg[8 * g + k, 40:48, :]
            total = total + labels
            acc = acc + pltpu.roll(jnp.where(slot_lane, labels, 0.0), (16 * k - 80) % 128, 1)
        index = acc.astype(jnp.int32)
        slot_v[8 * g : 8 * g + 8, :] = jnp.where(index == 0, SLOTS, index - 1)
    copy = pltpu.make_async_copy(slot_v, slot_s, sem)
    copy.start()

    def clear(k, carry):
        placed[pl.ds(pl.multiple_of(k * 64, 64), 64), :] = jnp.zeros((64, 128), jnp.float32)
        return carry

    lax.fori_loop(0, SLOTS // 64, clear, 0)
    copy.wait()

    def turn(p, tile):
        labels = msg[p, 40:48, :]
        for v in range(CAP // 8):
            own = msg[p, 8 * v : 8 * v + 8, :] if v < 6 else pltpu.roll(msg[p, 8 * v - 48 : 8 * v - 40, :], 64, 1)
            tile[8 * v : 8 * v + 8, :] = jnp.where(low, own, pltpu.roll(labels, (128 - v) % 128, 1) if v else labels)

    def spread(p, tile):
        row = p // 8 * 8
        col = p % 8 * 16
        for r in range(CAP):
            placed[pl.ds(slot_s[row + r % 8, col + r // 8], 1), :] = tile[r : r + 1, :]

    turn(0, tile_a)

    def step(k, carry):
        turn(2 * k + 1, tile_b)
        spread(2 * k, tile_a)
        turn(jnp.minimum(2 * k + 2, PEERS - 1), tile_a)
        spread(2 * k + 1, tile_b)
        return carry

    lax.fori_loop(0, PEERS // 2, step, 0)

    owned = iota((FOR_DEV, 128), 0)

    def finish(b, acc):
        view = placed[pl.ds(pl.multiple_of(b * 128, 128), 128), :].T
        x = view[:FIELDS]
        m = view[FIELDS : FIELDS + 1]
        blocks[:, b, :] = x
        block_mass[pl.ds(b, 1), :] = m
        where = view[96:97].astype(jnp.int32)
        member = (owned == where).astype(jnp.float32).astype(jnp.bfloat16)
        scaled = m * x
        terms = jnp.concatenate([scaled, scaled * x, jnp.broadcast_to(m, (8, 128))], axis=0)
        for _ in range(3):
            piece = terms.astype(jnp.bfloat16)
            terms = terms - piece.astype(jnp.float32)
            acc = acc + lax.dot_general(
                piece, member, (((1,), (1,)), ((), ())), preferred_element_type=jnp.float32
            )
        return acc

    acc = lax.fori_loop(0, BLK_DEV, finish, jnp.zeros((2 * FIELDS + 8, FOR_DEV), jnp.float32))
    weight = acc[2 * FIELDS : 2 * FIELDS + 1]
    mass_total = jnp.broadcast_to(total[0:1, 127:128], (1, FOR_DEV))
    fmass[...] = weight * (FOR_DEV * PEERS / mass_total)
    fmean[...] = acc[:FIELDS] / weight
    fsecond[...] = acc[FIELDS : 2 * FIELDS] / weight


def pack(records, halo_mass, forest_id, dest_block, dest_slot):
    groups = halo_mass.size // 128
    return pl.pallas_call(
        pack_kernel,
        out_shape=jax.ShapeDtypeStruct((PEERS, ROWS, 128), jnp.float32),
        in_specs=[pl.BlockSpec(memory_space=pltpu.VMEM)] * 5,
        out_specs=pl.BlockSpec(memory_space=pltpu.VMEM),
        scratch_shapes=[
            pltpu.VMEM((PEERS * CAP, 128), jnp.float32),
            pltpu.VMEM((128, 128), jnp.float32),
            pltpu.VMEM((128, 128), jnp.float32),
            pltpu.VMEM((groups, 128), jnp.int32),
            pltpu.SMEM((groups, 128), jnp.int32),
            pltpu.SemaphoreType.DMA,
        ],
        name="pack",
    )(records, halo_mass, forest_id, dest_block, dest_slot)


def place(msg):
    f32 = jnp.float32
    return pl.pallas_call(
        place_kernel,
        out_shape=(
            jax.ShapeDtypeStruct((FIELDS, BLK_DEV, 128), f32),
            jax.ShapeDtypeStruct((BLK_DEV, 128), f32),
            jax.ShapeDtypeStruct((1, FOR_DEV), f32),
            jax.ShapeDtypeStruct((FIELDS, FOR_DEV), f32),
            jax.ShapeDtypeStruct((FIELDS, FOR_DEV), f32),
        ),
        in_specs=[pl.BlockSpec(memory_space=pltpu.VMEM)],
        out_specs=(pl.BlockSpec(memory_space=pltpu.VMEM),) * 5,
        scratch_shapes=[
            pltpu.VMEM((SLOTS + 8, 128), f32),
            pltpu.VMEM((CAP, 128), f32),
            pltpu.VMEM((CAP, 128), f32),
            pltpu.VMEM((PEERS, 128), jnp.int32),
            pltpu.SMEM((PEERS, 128), jnp.int32),
            pltpu.SemaphoreType.DMA,
        ],
        name="place",
    )(msg)


def on_device(records, halo_mass, forest_id, dest_block, dest_slot):
    outbox = pack(records, halo_mass, forest_id, dest_block, dest_slot)
    inbox = lax.all_to_all(outbox, SA_HA, split_axis=0, concat_axis=0, tiled=True)
    blocks, block_mass, fmass, fmean, fsecond = place(inbox)
    return blocks, block_mass, fmass.reshape(FOR_DEV), fmean, fsecond


def solution(mesh):
    split = Mesh(
        mesh.devices.reshape(mesh.shape["row"], mesh.shape["sa"], 8, 2),
        ("row", "sa", "ha_0", "ha_1"),
    )
    in_specs = (
        P(None, "sa", ROW_HA),
        P("sa", ROW_HA),
        P("sa", ROW_HA),
        P("sa", ROW_HA),
        P("sa", ROW_HA),
    )
    out_specs = (
        P(None, ROW_SA_HA, None),
        P(ROW_SA_HA, None),
        P(ROW_SA_HA),
        P(None, ROW_SA_HA),
        P(None, ROW_SA_HA),
    )
    return jax.shard_map(
        on_device, mesh=split, in_specs=in_specs, out_specs=out_specs, check_vma=False
    )
```

time: 214 us -> 94.7 us (0.44)
  matrix products: 77.7 us -> 0 us
  Pallas kernels: 0 us -> 41 us
  local copies, waits for them, and re-layouts: 31.9 us -> 0 us
  loops' own time: 14.1 us -> 0 us
  blocking collectives: 66.7 us -> 52.9 us
  starting transfers between devices: 13.1 us -> 0 us
  other arithmetic: 8.31 us -> 0 us
    dot_general x24 -> x0, matrix products: 77.7 us -> none  [the longest x21 75 us: one_tile(): jnp.dot(source, select, precision=lax.Precision.HIGHEST, preferred_elemen...]
    psum x3 -> x0, blocking collectives: 66.7 us -> none  [by_axis(): array = lax.psum(array, axis)]
    all_to_all x0 -> x1, blocking collectives: none -> 52.9 us  [on_device(): lax.all_to_all(outbox, SA_HA, split_axis=0, concat_axis=0, tiled=True)]
    pallas_call x0 -> x2, Pallas kernels: none -> 41 us  [the longest x1 27.6 us: place(): pl.pallas_call(place_kernel, out_shape=(jax.ShapeDtypeStruct((FIELDS, BLK...]
    another operation x2 -> x0, loops' own time: 14.1 us -> none  [tiled_place(): pieces = lax.map(one_tile, jnp.arange(tile_count, dtype=jnp.int32))]
    all_to_all x1 -> x0, starting transfers between devices: 13.1 us -> none  [in_one_piece(): lax.all_to_all(both, axis, split_axis=split_dim, concat_axis=concat_dim,...]
    dynamic_slice x21 -> x0, local copies, waits for them, and re-layouts: 12.3 us -> none  [tiled_place(): pieces = lax.map(one_tile, jnp.arange(tile_count, dtype=jnp.int32))]
    reshape x4 -> x0, local copies, waits for them, and re-layouts: 8.6 us -> none  [the longest x1 3.35 us: on_device(): incoming = arrived[0].reshape(fields, width_out)]
  transfers between devices with their start and end apart: 1 -> 0, of which waited for: 0 -> 0; matrix products, arithmetic and copies ran while one was open for 0% -> 0% of each run, Pallas kernels for 0% -> 0%
where the time goes in v1:
time: 94.7 us; the launch traced here: 94.5 us
  blocking collectives  52.9 us (56%)
  Pallas kernels  41 us (43%)
    all_to_all x1, blocking collectives, on_device(): lax.all_to_all(outbox, SA_HA, split_axis=0, concat_axis=0, tiled=True)  52.9 us
    pallas_call x1, Pallas kernels, place(): pl.pallas_call(place_kernel, out_shape=(jax.ShapeDtypeStruct((FIELDS, BLK...  27.6 us
    pallas_call x1, Pallas kernels, pack(): pl.pallas_call(pack_kernel, out_shape=jax.ShapeDtypeStruct((PEERS, ROWS,...  13.4 us

profile of v1, /device:TPU:1, one launch (start us, length us, event | category | flops | bytes accessed | tf_op | source)
XLA Modules:
  0.0 94.5 jit_solution(4197290508338895940)
XLA Ops:
  0.6 13.4 %pack.1 = f32[64,48,128]{2,1,0:T(8,128)} custom-call(f32[64,4,1024]{2,1,0:T(4,128)} %rec.1, f32[4,1024]{1,0:T(4,128)} %mass.1, s32[4,1024]{1,0:T(4,128)} %forest.1, s32[4,1024]{1,0:T(4,128)} %block.1, s32[4,1024]{1,0:T(4,128)} %slot.1), custom_call_target="tpu_custom_call" | custom-call | tf_op jit(solution)/shard_map/pack/pallas_call | solution.py:207
  14.1 52.9 %all_to_all.5.msg = f32[64,48,128]{2,1,0:T(8,128)} all-to-all(f32[64,48,128]{2,1,0:T(8,128)} %pack.1), channel_id=1, replica_groups=mesh['row'=4,'sa'=4,'ha_0'=8,'ha_1'=2] {'sa','ha_0','ha_1'}, dimensions={0} | all-to-all | bytes 3145728 | tf_op jit(solution)/shard_map/all_to_all | solution.py:251
  66.9 27.6 %place.1 = (f32[64,40,128]{2,1,0:T(8,128)}, f32[40,128]{1,0:T(8,128)}, f32[1,128]{1,0:T(1,128)}, f32[64,128]{1,0:T(8,128)}, f32[64,128]{1,0:T(8,128)}) custom-call(f32[64,48,128]{2,1,0:T(8,128)} %all_to_all.5.msg), custom_call_target="tpu_custom_call" | custom-call | tf_op jit(solution)/shard_map/place/pallas_call | solution.py:226

commit v2 on v1

v2 whole, which is shorter than its diff:
```python
import jax
import jax.numpy as jnp
from jax import lax
from jax.experimental import pallas as pl
from jax.experimental.pallas import tpu as pltpu
from jax.sharding import Mesh
from jax.sharding import PartitionSpec as P

FIELDS = 64
FOR_DEV = 128
BLK_DEV = 40
SLOTS = BLK_DEV * 128
PEERS = 64
CAP = 88
ROWS = 48
VMEM_LIMIT = 24 * 1024 * 1024
EXCHANGE = ("core", "sa", "z0", "z1", "z2")
ROW_HA = ("row", "z2", "z1", "z0", "core")
ROW_SA_HA = ("row", "sa", "z2", "z1", "z0", "core")


def iota(shape, dim):
    return lax.broadcasted_iota(jnp.int32, shape, dim)


def owner_of(block):
    return lax.shift_right_logical(block * 1639, 16)


def position_of(owner):
    core = (owner & 1) << 5
    plane = lax.shift_right_logical(owner, 4) << 3
    turned = ((owner & 2) << 1) | lax.shift_right_logical(owner & 4, 1) | lax.shift_right_logical(owner & 8, 3)
    return core | plane | turned


def pack_kernel(
    rec_hbm, mass, forest, block, slot, out, placed, rec, labels, tiles, target_v, target_s, rec_sem, sems
):
    snaps, halos = mass.shape
    groups = snaps * halos // 128
    rec_copy = pltpu.make_async_copy(rec_hbm, rec, rec_sem)
    rec_copy.start()
    before = (iota((256, 384), 0) < iota((256, 384), 1)) | (iota((256, 384), 1) >= 256)
    before = before.astype(jnp.float32).astype(jnp.bfloat16)
    peer = iota((PEERS, 256), 0)
    base = jnp.zeros((PEERS, 128), jnp.float32)
    line = iota((8, 128), 0)

    for q in range(halos // 256):
        for s in range(snaps):
            cols = slice(256 * q, 256 * q + 256)
            blk = block[s : s + 1, cols]
            own = owner_of(blk)
            place = position_of(own)
            member = peer == place
            counts = jnp.dot(
                member.astype(jnp.float32).astype(jnp.bfloat16), before, preferred_element_type=jnp.float32
            )
            rank = counts[:, :256] + jnp.concatenate([base, base], axis=1)
            rank = jnp.sum(jnp.where(member, rank, 0.0), axis=0, keepdims=True)
            base = base + counts[:, 256:]
            target = place * CAP + rank.astype(jnp.int32)
            local = ((blk - own * BLK_DEV) * 128 + slot[s : s + 1, cols] + 1).astype(jnp.float32)
            here = (forest[s : s + 1, cols] & (FOR_DEV - 1)).astype(jnp.float32)
            heavy = mass[s : s + 1, cols]
            for h in range(2):
                part = slice(128 * h, 128 * h + 128)
                group = 8 * q + 4 * h + s
                target_v[group : group + 1, :] = target[:, part]
                tile = jnp.where(line == 0, jnp.broadcast_to(heavy[:, part], (8, 128)), 0.0)
                tile = jnp.where(line == 1, jnp.broadcast_to(local[:, part], (8, 128)), tile)
                tile = jnp.where(line == 2, jnp.broadcast_to(here[:, part], (8, 128)), tile)
                labels[8 * group : 8 * group + 8, :] = tile

    def index_copy(k, buf):
        return pltpu.make_async_copy(
            target_v.at[pl.ds(pl.multiple_of(8 * k, 8), 8), :], target_s[buf], sems.at[buf]
        )

    index_copy(0, 0).start()
    index_copy(1, 1).start()
    for tile in tiles:
        tile[...] = jnp.zeros_like(tile)

    def clear(k, carry):
        placed[pl.ds(pl.multiple_of(k * 128, 128), 128), :] = jnp.zeros((128, 128), jnp.float32)
        return carry

    lax.fori_loop(0, PEERS * CAP // 128, clear, 0)
    rec_copy.wait()

    def turn(group, tile):
        stack = jnp.concatenate(
            [
                rec[pl.ds(group, FIELDS, stride=groups), :],
                labels[pl.ds(pl.multiple_of(8 * group, 8), 8), :],
            ],
            axis=0,
        )
        tile[:, : FIELDS + 8] = stack.T

    turn(0, tiles[0])

    def step(k, carry):
        for i in range(16):
            if i % 8 == 0:
                index_copy(0, i // 8).wait()
            after = jnp.minimum(16 * k + i + 1, groups - 1)
            turn(after, tiles[(i + 1) % 4])
            tile = tiles[i % 4]
            for r in range(128):
                placed[pl.ds(target_s[i // 8][i % 8, r], 1), :] = tile[r : r + 1, :]
            if i % 8 == 7:

                @pl.when(2 * k + i // 8 + 2 < groups // 8)
                def _():
                    index_copy(2 * k + i // 8 + 2, i // 8).start()

        return carry

    lax.fori_loop(0, groups // 16, step, 0)

    lane = iota((8, 128), 1)
    low = lane < FIELDS
    total = jnp.sum(jnp.sum(mass[...], axis=0, keepdims=True), axis=1, keepdims=True)
    corner = jnp.where(lane == 127, jnp.broadcast_to(total, (8, 128)), 0.0)

    def squeeze(k, carry):
        for h in range(4):
            p = 4 * k + h
            start = p * CAP
            rows = [placed[pl.ds(pl.multiple_of(start + 8 * v, 8), 8), :] for v in range(CAP // 8)]
            tags = corner
            for v in range(CAP // 8):
                own = jnp.where(low, 0.0, rows[v])
                tags = tags + (pltpu.roll(own, 4 * v, 1) if v else own)
            for v in range(5):
                out[p, 8 * v : 8 * v + 8, :] = jnp.where(low, rows[v], pltpu.roll(rows[v + 6], 64, 1))
            out[p, 40:48, :] = jnp.where(low, rows[5], tags)
        return carry

    lax.fori_loop(0, PEERS // 4, squeeze, 0)


def place_kernel(
    msg, blocks, block_mass, fmass, fmean, fsecond, placed, acc, tiles, slot_v, slot_s, sems
):
    lane = iota((8, 128), 1)
    low = lane < FIELDS
    slot_lane = (lane >= FIELDS) & (lane < FIELDS + 4 * (CAP // 8)) & (lane % 4 == 1)
    total = jnp.zeros((8, 128), jnp.float32)
    for g in range(PEERS // 8):
        index = jnp.zeros((8, 128), jnp.float32)
        for k in range(8):
            tags = msg[8 * g + k, 40:48, :]
            total = total + tags
            index = index + pltpu.roll(
                jnp.where(slot_lane, tags, 0.0), (64 * (k // 4) + k % 4 - 65) % 128, 1
            )
        index = index.astype(jnp.int32)
        slot_v[8 * g : 8 * g + 8, :] = jnp.where(index == 0, SLOTS, index - 1)

    def index_copy(g, buf):
        return pltpu.make_async_copy(
            slot_v.at[pl.ds(pl.multiple_of(8 * g, 8), 8), :], slot_s[buf], sems.at[buf]
        )

    index_copy(0, 0).start()
    index_copy(1, 1).start()

    def clear(k, carry):
        placed[pl.ds(pl.multiple_of(k * 128, 128), 128), :] = jnp.zeros((128, 128), jnp.float32)
        return carry

    lax.fori_loop(0, SLOTS // 128, clear, 0)
    acc[...] = jnp.zeros_like(acc)

    def turn(p, tile):
        tags = msg[p, 40:48, :]
        for v in range(CAP // 8):
            if v < 6:
                own = msg[p, 8 * v : 8 * v + 8, :]
            else:
                own = pltpu.roll(msg[p, 8 * v - 48 : 8 * v - 40, :], 64, 1)
            side = pltpu.roll(tags, 128 - 4 * v, 1) if v else tags
            tile[8 * v : 8 * v + 8, :] = jnp.where(low, own, side)

    turn(0, tiles[0])

    def step(k, carry):
        for i in range(16):
            if i % 8 == 0:
                index_copy(0, i // 8).wait()
            turn(jnp.minimum(16 * k + i + 1, PEERS - 1), tiles[(i + 1) % 4])
            tile = tiles[i % 4]
            for r in range(CAP):
                col = r // 8 * 4 + i % 8 % 4 + i % 8 // 4 * 64
                placed[pl.ds(slot_s[i // 8][r % 8, col], 1), :] = tile[r : r + 1, :]
            if i % 8 == 7:

                @pl.when(2 * k + i // 8 + 2 < PEERS // 8)
                def _():
                    index_copy(2 * k + i // 8 + 2, i // 8).start()

        return carry

    lax.fori_loop(0, PEERS // 16, step, 0)

    owned = iota((FOR_DEV, 128), 0)

    def finish(k, carry):
        highs, lows, members = [], [], []
        for h in range(4):
            b = 4 * k + h
            view = placed[pl.ds(pl.multiple_of(b * 128, 128), 128), :].T
            x = view[:FIELDS]
            m = view[FIELDS : FIELDS + 1]
            blocks[pl.ds(b, FIELDS, stride=BLK_DEV), :] = x
            block_mass[pl.ds(b, 1), :] = m
            forest = view[FIELDS + 2 : FIELDS + 3].astype(jnp.int32)
            members.append((owned == forest).astype(jnp.float32).astype(jnp.bfloat16))
            scaled = m * x
            terms = jnp.concatenate([scaled, scaled * x, jnp.broadcast_to(m, (8, 128))], axis=0)
            high = terms.astype(jnp.bfloat16)
            highs.append(high)
            lows.append((terms - high.astype(jnp.float32)).astype(jnp.bfloat16))
        member = jnp.concatenate(members, axis=1)
        for part in (highs, lows):
            acc[...] += lax.dot_general(
                jnp.concatenate(part, axis=1),
                member,
                (((1,), (1,)), ((), ())),
                preferred_element_type=jnp.float32,
            )
        return carry

    lax.fori_loop(0, BLK_DEV // 4, finish, 0)
    weight = acc[2 * FIELDS : 2 * FIELDS + 1]
    mass_total = jnp.broadcast_to(total[0:1, 127:128], (1, FOR_DEV))
    fmass[...] = weight * (FOR_DEV * PEERS / mass_total)
    fmean[...] = acc[:FIELDS] / weight
    fsecond[...] = acc[FIELDS : 2 * FIELDS] / weight


def pack(records, halo_mass, forest_id, dest_block, dest_slot):
    snaps, halos = halo_mass.shape
    groups = snaps * halos // 128
    by_group = records.reshape(FIELDS, snaps, halos // 128, 128).transpose(0, 2, 1, 3)
    by_group = by_group.reshape(FIELDS * groups, 128)
    vmem = pl.BlockSpec(memory_space=pltpu.VMEM)
    return pl.pallas_call(
        pack_kernel,
        out_shape=jax.ShapeDtypeStruct((PEERS, ROWS, 128), jnp.float32),
        in_specs=[pl.BlockSpec(memory_space=pl.ANY)] + [vmem] * 4,
        out_specs=vmem,
        scratch_shapes=[
            pltpu.VMEM((PEERS * CAP, 128), jnp.float32),
            pltpu.VMEM((FIELDS * groups, 128), jnp.float32),
            pltpu.VMEM((8 * groups, 128), jnp.float32),
            [pltpu.VMEM((128, 128), jnp.float32)] * 4,
            pltpu.VMEM((groups, 128), jnp.int32),
            [pltpu.SMEM((8, 128), jnp.int32)] * 2,
            pltpu.SemaphoreType.DMA,
            pltpu.SemaphoreType.DMA((2,)),
        ],
        compiler_params=pltpu.CompilerParams(vmem_limit_bytes=VMEM_LIMIT),
        name="pack",
    )(by_group, halo_mass, forest_id, dest_block, dest_slot)


def place(msg):
    f32 = jnp.float32
    vmem = pl.BlockSpec(memory_space=pltpu.VMEM)
    return pl.pallas_call(
        place_kernel,
        out_shape=(
            jax.ShapeDtypeStruct((FIELDS * BLK_DEV, 128), f32),
            jax.ShapeDtypeStruct((BLK_DEV, 128), f32),
            jax.ShapeDtypeStruct((1, FOR_DEV), f32),
            jax.ShapeDtypeStruct((FIELDS, FOR_DEV), f32),
            jax.ShapeDtypeStruct((FIELDS, FOR_DEV), f32),
        ),
        in_specs=[vmem],
        out_specs=(vmem,) * 5,
        scratch_shapes=[
            pltpu.VMEM((SLOTS + 8, 128), f32),
            pltpu.VMEM((2 * FIELDS + 8, FOR_DEV), f32),
            [pltpu.VMEM((CAP, 128), f32)] * 4,
            pltpu.VMEM((PEERS, 128), jnp.int32),
            [pltpu.SMEM((8, 128), jnp.int32)] * 2,
            pltpu.SemaphoreType.DMA((2,)),
        ],
        compiler_params=pltpu.CompilerParams(vmem_limit_bytes=VMEM_LIMIT),
        name="place",
    )(msg)


def on_device(records, halo_mass, forest_id, dest_block, dest_slot):
    outbox = pack(records, halo_mass, forest_id, dest_block, dest_slot)
    inbox = lax.all_to_all(outbox, EXCHANGE, split_axis=0, concat_axis=0, tiled=True)
    blocks, block_mass, fmass, fmean, fsecond = place(inbox)
    return blocks.reshape(FIELDS, BLK_DEV, 128), block_mass, fmass.reshape(FOR_DEV), fmean, fsecond


def solution(mesh):
    split = Mesh(
        mesh.devices.reshape(mesh.shape["row"], mesh.shape["sa"], 2, 2, 2, 2),
        ROW_SA_HA,
    )
    in_specs = (
        P(None, "sa", ROW_HA),
        P("sa", ROW_HA),
        P("sa", ROW_HA),
        P("sa", ROW_HA),
        P("sa", ROW_HA),
    )
    out_specs = (
        P(None, ROW_SA_HA, None),
        P(ROW_SA_HA, None),
        P(ROW_SA_HA),
        P(None, ROW_SA_HA),
        P(None, ROW_SA_HA),
    )
    return jax.shard_map(
        on_device, mesh=split, in_specs=in_specs, out_specs=out_specs, check_vma=False
    )
```

time: 94.7 us -> 72.9 us (0.77)
  Pallas kernels: 41 us -> 15.6 us
  local copies, waits for them, and re-layouts: 0 us -> 4.09 us
    pallas_call x1, Pallas kernels: 27.6 us -> 9.26 us  [place(): pl.pallas_call(place_kernel, out_shape=(jax.ShapeDtypeStruct((FIELDS * BL...]
    pallas_call x1, Pallas kernels: 13.4 us -> 6.38 us  [pack(): pl.pallas_call(pack_kernel, out_shape=jax.ShapeDtypeStruct((PEERS, ROWS,...]
    unnamed x0 -> x10, local copies, waits for them, and re-layouts: none -> 4.09 us
where the time goes in v2:
time: 72.9 us; the launch traced here: 72.4 us
  blocking collectives  52 us (71%)
  Pallas kernels  15.6 us (21%)
  local copies, waits for them, and re-layouts  4.09 us (6%)
    all_to_all x1, blocking collectives, on_device(): lax.all_to_all(outbox, EXCHANGE, split_axis=0, concat_axis=0, tiled=True)  52 us
    pallas_call x1, Pallas kernels, place(): pl.pallas_call(place_kernel, out_shape=(jax.ShapeDtypeStruct((FIELDS * BL...  9.26 us
    pallas_call x1, Pallas kernels, pack(): pl.pallas_call(pack_kernel, out_shape=jax.ShapeDtypeStruct((PEERS, ROWS,...  6.38 us
    unnamed x10, local copies, waits for them, and re-layouts  4.09 us

profile of v2, /device:TPU:1, one launch (start us, length us, event | category | flops | bytes accessed | tf_op | source)
XLA Modules:
  0.0 72.4 jit_solution(6454855241706005730)
XLA Ops:
  0.6 0.0 copy-start
  0.6 1.2 %copy-done = f32[64,4,1024]{2,1,0:T(4,128)S(1)} copy-done((f32[64,4,1024]{2,1,0:T(4,128)S(1)}, f32[64,4,1024]{2,1,0:T(4,128)}, u32[]{:S(2)}) %copy-start) | copy-done | bytes 1048600
  1.9 0.0 copy-start.1
  1.9 0.7 copy-done.1
  2.6 0.0 copy-start.2
  2.6 0.7 copy-done.2
  3.3 0.0 copy-start.3
  3.3 0.7 copy-done.3
  4.0 0.0 copy-start.4
  4.0 0.7 copy-done.4
  4.7 6.4 %pack.1 = f32[64,48,128]{2,1,0:T(8,128)S(1)} custom-call(f32[2048,128]{1,0:T(8,128)S(1)} %bitcast.7, f32[4,1024]{1,0:T(4,128)S(1)} %copy-done.1, s32[4,1024]{1,0:T(4,128)S(1)} %copy-done.2, s32[4,1024]{1,0:T(4,128)S(1)} %copy-done.3, s32[4,1024]{1,0:T(4,128)S(1)} %copy-done.4), custom_call_target="tpu_custom_call" | custom-call | tf_op jit(solution)/shard_map/pack/pallas_call | solution.py:252
  11.1 52.0 %all_to_all.5.msg = f32[64,48,128]{2,1,0:T(8,128)S(1)} all-to-all(f32[64,48,128]{2,1,0:T(8,128)S(1)} %pack.1), channel_id=1, replica_groups=mesh['row'=4,'sa'=4,'z2'=2,'z1'=2,'z0'=2,'core'=2] {'core','sa','z0','z1..., dimensions={0} | all-to-all | bytes 3145728 | tf_op jit(solution)/shard_map/all_to_all | solution.py:301
  63.1 9.3 %place.1 = (f32[2560,128]{1,0:T(8,128)}, f32[40,128]{1,0:T(8,128)}, f32[1,128]{1,0:T(1,128)}, f32[64,128]{1,0:T(8,128)}, f32[64,128]{1,0:T(8,128)}) custom-call(f32[64,48,128]{2,1,0:T(8,128)S(1)} %all_to_all.5.msg), custom_call_target="tpu_custom_call" | custom-call | tf_op jit(solution)/shard_map/place/pallas_call | solution.py:275
Async XLA Ops:
  0.6 1.2 %copy-start = (f32[64,4,1024]{2,1,0:T(4,128)S(1)}, f32[64,4,1024]{2,1,0:T(4,128)}, u32[]{:S(2)}) copy-start(f32[64,4,1024]{2,1,0:T(4,128)} %param.5) | copy-start | bytes 3145732
  1.9 0.7 copy-start.1
  2.6 0.7 copy-start.2
  3.3 0.7 copy-start.3
  4.0 0.7 copy-start.4

commit v3 on v2

--- a/solution.py
+++ b/solution.py
@@ -13,6 +13,7 @@
 PEERS = 64
 CAP = 88
 ROWS = 48
+TAGS = 48
 VMEM_LIMIT = 24 * 1024 * 1024
 EXCHANGE = ("core", "sa", "z0", "z1", "z2")
 ROW_HA = ("row", "z2", "z1", "z0", "core")
@@ -34,44 +35,32 @@
     return core | plane | turned
 
 
-def pack_kernel(
-    rec_hbm, mass, forest, block, slot, out, placed, rec, labels, tiles, target_v, target_s, rec_sem, sems
-):
-    snaps, halos = mass.shape
-    groups = snaps * halos // 128
-    rec_copy = pltpu.make_async_copy(rec_hbm, rec, rec_sem)
-    rec_copy.start()
+def rank_kernel(block, target, first_tag):
+    groups = block.shape[0]
     before = (iota((256, 384), 0) < iota((256, 384), 1)) | (iota((256, 384), 1) >= 256)
     before = before.astype(jnp.float32).astype(jnp.bfloat16)
-    peer = iota((PEERS, 256), 0)
+    peer = iota((PEERS, 128), 0)
     base = jnp.zeros((PEERS, 128), jnp.float32)
-    line = iota((8, 128), 0)
-
-    for q in range(halos // 256):
-        for s in range(snaps):
-            cols = slice(256 * q, 256 * q + 256)
-            blk = block[s : s + 1, cols]
-            own = owner_of(blk)
-            place = position_of(own)
-            member = peer == place
-            counts = jnp.dot(
-                member.astype(jnp.float32).astype(jnp.bfloat16), before, preferred_element_type=jnp.float32
-            )
-            rank = counts[:, :256] + jnp.concatenate([base, base], axis=1)
-            rank = jnp.sum(jnp.where(member, rank, 0.0), axis=0, keepdims=True)
-            base = base + counts[:, 256:]
-            target = place * CAP + rank.astype(jnp.int32)
-            local = ((blk - own * BLK_DEV) * 128 + slot[s : s + 1, cols] + 1).astype(jnp.float32)
-            here = (forest[s : s + 1, cols] & (FOR_DEV - 1)).astype(jnp.float32)
-            heavy = mass[s : s + 1, cols]
-            for h in range(2):
-                part = slice(128 * h, 128 * h + 128)
-                group = 8 * q + 4 * h + s
-                target_v[group : group + 1, :] = target[:, part]
-                tile = jnp.where(line == 0, jnp.broadcast_to(heavy[:, part], (8, 128)), 0.0)
-                tile = jnp.where(line == 1, jnp.broadcast_to(local[:, part], (8, 128)), tile)
-                tile = jnp.where(line == 2, jnp.broadcast_to(here[:, part], (8, 128)), tile)
-                labels[8 * group : 8 * group + 8, :] = tile
+    goal = position_of(owner_of(block[...]))
+    for g in range(0, groups, 2):
+        member = jnp.concatenate([peer == goal[g : g + 1], peer == goal[g + 1 : g + 2]], axis=1)
+        counts = jnp.dot(
+            member.astype(jnp.float32).astype(jnp.bfloat16), before, preferred_element_type=jnp.float32
+        )
+        rank = counts[:, :256] + jnp.concatenate([base, base], axis=1)
+        rank = jnp.sum(jnp.where(member, rank, 0.0), axis=0, keepdims=True).astype(jnp.int32)
+        base = base + counts[:, 256:]
+        first_tag[g : g + 1, :] = rank[:, :128]
+        first_tag[g + 1 : g + 2, :] = rank[:, 128:]
+    rank = first_tag[...]
+    target[...] = goal * CAP + rank
+    first_tag[...] = lax.shift_right_logical(rank, 3) << 2
+
+
+def pack_kernel(
+    target_v, first_tag, rec, mass, forest, block, slot_in, out, placed, slot, tiles, target_s, sems
+):
+    groups = mass.shape[0]
 
     def index_copy(k, buf):
         return pltpu.make_async_copy(
@@ -82,23 +71,25 @@
     index_copy(1, 1).start()
     for tile in tiles:
         tile[...] = jnp.zeros_like(tile)
+    slot[...] = (block[...] - owner_of(block[...]) * BLK_DEV) * 128 + slot_in[...] + 1
 
     def clear(k, carry):
         placed[pl.ds(pl.multiple_of(k * 128, 128), 128), :] = jnp.zeros((128, 128), jnp.float32)
         return carry
 
     lax.fori_loop(0, PEERS * CAP // 128, clear, 0)
-    rec_copy.wait()
+    line = iota((TAGS, 128), 0)
 
     def turn(group, tile):
-        stack = jnp.concatenate(
-            [
-                rec[pl.ds(group, FIELDS, stride=groups), :],
-                labels[pl.ds(pl.multiple_of(8 * group, 8), 8), :],
-            ],
-            axis=0,
-        )
-        tile[:, : FIELDS + 8] = stack.T
+        def row(ref):
+            return jnp.broadcast_to(ref[pl.ds(group, 1), :], (TAGS, 128))
+
+        own_line = line - row(first_tag)
+        tags = jnp.where(own_line == 0, row(mass), 0.0)
+        tags = jnp.where(own_line == 1, row(slot).astype(jnp.float32), tags)
+        tags = jnp.where(own_line == 2, (row(forest) & (FOR_DEV - 1)).astype(jnp.float32), tags)
+        stack = jnp.concatenate([rec[pl.ds(group, FIELDS, stride=groups), :], tags], axis=0)
+        tile[:, : FIELDS + TAGS] = stack.T
 
     turn(0, tiles[0])
 
@@ -127,25 +118,25 @@
     corner = jnp.where(lane == 127, jnp.broadcast_to(total, (8, 128)), 0.0)
 
     def squeeze(k, carry):
-        for h in range(4):
-            p = 4 * k + h
+        for h in range(8):
+            p = 8 * k + h
             start = p * CAP
             rows = [placed[pl.ds(pl.multiple_of(start + 8 * v, 8), 8), :] for v in range(CAP // 8)]
-            tags = corner
-            for v in range(CAP // 8):
-                own = jnp.where(low, 0.0, rows[v])
-                tags = tags + (pltpu.roll(own, 4 * v, 1) if v else own)
             for v in range(5):
                 out[p, 8 * v : 8 * v + 8, :] = jnp.where(low, rows[v], pltpu.roll(rows[v + 6], 64, 1))
+            tags = corner
+            for row in rows:
+                tags = tags + row
             out[p, 40:48, :] = jnp.where(low, rows[5], tags)
         return carry
 
-    lax.fori_loop(0, PEERS // 4, squeeze, 0)
+    lax.fori_loop(0, PEERS // 8, squeeze, 0)
 
 
 def place_kernel(
-    msg, blocks, block_mass, fmass, fmean, fsecond, placed, acc, tiles, slot_v, slot_s, sems
+    msg, blocks_hbm, block_mass, fmass, fmean, fsecond, blocks, placed, acc, tiles, slot_v, slot_s, sems, out_sems
 ):
+    by_row = blocks.reshape(FIELDS * BLK_DEV, 128)
     lane = iota((8, 128), 1)
     low = lane < FIELDS
     slot_lane = (lane >= FIELDS) & (lane < FIELDS + 4 * (CAP // 8)) & (lane % 4 == 1)
@@ -209,14 +200,18 @@
 
     owned = iota((FOR_DEV, 128), 0)
 
+    def out_copy(k):
+        part = pl.ds(8 * k if isinstance(k, int) else pl.multiple_of(8 * k, 8), 8)
+        return pltpu.make_async_copy(blocks.at[:, part, :], blocks_hbm.at[:, part, :], out_sems.at[k])
+
     def finish(k, carry):
         highs, lows, members = [], [], []
-        for h in range(4):
-            b = 4 * k + h
+        for h in range(8):
+            b = 8 * k + h
             view = placed[pl.ds(pl.multiple_of(b * 128, 128), 128), :].T
             x = view[:FIELDS]
             m = view[FIELDS : FIELDS + 1]
-            blocks[pl.ds(b, FIELDS, stride=BLK_DEV), :] = x
+            by_row[pl.ds(b, FIELDS, stride=BLK_DEV), :] = x
             block_mass[pl.ds(b, 1), :] = m
             forest = view[FIELDS + 2 : FIELDS + 3].astype(jnp.int32)
             members.append((owned == forest).astype(jnp.float32).astype(jnp.bfloat16))
@@ -225,6 +220,7 @@
             high = terms.astype(jnp.bfloat16)
             highs.append(high)
             lows.append((terms - high.astype(jnp.float32)).astype(jnp.bfloat16))
+        out_copy(k).start()
         member = jnp.concatenate(members, axis=1)
         for part in (highs, lows):
             acc[...] += lax.dot_general(
@@ -235,38 +231,53 @@
             )
         return carry
 
-    lax.fori_loop(0, BLK_DEV // 4, finish, 0)
+    lax.fori_loop(0, BLK_DEV // 8, finish, 0)
     weight = acc[2 * FIELDS : 2 * FIELDS + 1]
     mass_total = jnp.broadcast_to(total[0:1, 127:128], (1, FOR_DEV))
     fmass[...] = weight * (FOR_DEV * PEERS / mass_total)
     fmean[...] = acc[:FIELDS] / weight
     fsecond[...] = acc[FIELDS : 2 * FIELDS] / weight
+    for k in range(BLK_DEV // 8):
+        out_copy(k).wait()
 
 
 def pack(records, halo_mass, forest_id, dest_block, dest_slot):
     snaps, halos = halo_mass.shape
     groups = snaps * halos // 128
-    by_group = records.reshape(FIELDS, snaps, halos // 128, 128).transpose(0, 2, 1, 3)
-    by_group = by_group.reshape(FIELDS * groups, 128)
+
+    def by_group(a):
+        lead = a.shape[:-2]
+        a = a.reshape(lead + (snaps, halos // 128, 128))
+        return jnp.swapaxes(a, -3, -2).reshape(-1, 128)
+
+    records, mass, forest, block, slot = map(by_group, (records, halo_mass, forest_id, dest_block, dest_slot))
+    row = (groups, 128)
     vmem = pl.BlockSpec(memory_space=pltpu.VMEM)
+    params = pltpu.CompilerParams(vmem_limit_bytes=VMEM_LIMIT)
+    target, first_tag = pl.pallas_call(
+        rank_kernel,
+        out_shape=(jax.ShapeDtypeStruct(row, jnp.int32),) * 2,
+        in_specs=[vmem],
+        out_specs=(vmem,) * 2,
+        cost_estimate=pl.CostEstimate(flops=2**31, bytes_accessed=2**16, transcendentals=0),
+        compiler_params=params,
+        name="rank",
+    )(block)
     return pl.pallas_call(
         pack_kernel,
         out_shape=jax.ShapeDtypeStruct((PEERS, ROWS, 128), jnp.float32),
-        in_specs=[pl.BlockSpec(memory_space=pl.ANY)] + [vmem] * 4,
+        in_specs=[vmem] * 7,
         out_specs=vmem,
         scratch_shapes=[
             pltpu.VMEM((PEERS * CAP, 128), jnp.float32),
-            pltpu.VMEM((FIELDS * groups, 128), jnp.float32),
-            pltpu.VMEM((8 * groups, 128), jnp.float32),
+            pltpu.VMEM(row, jnp.int32),
             [pltpu.VMEM((128, 128), jnp.float32)] * 4,
-            pltpu.VMEM((groups, 128), jnp.int32),
             [pltpu.SMEM((8, 128), jnp.int32)] * 2,
-            pltpu.SemaphoreType.DMA,
             pltpu.SemaphoreType.DMA((2,)),
         ],
-        compiler_params=pltpu.CompilerParams(vmem_limit_bytes=VMEM_LIMIT),
+        compiler_params=params,
         name="pack",
-    )(by_group, halo_mass, forest_id, dest_block, dest_slot)
+    )(target, first_tag, records, mass, forest, block, slot)
 
 
 def place(msg):
@@ -275,21 +286,23 @@
     return pl.pallas_call(
         place_kernel,
         out_shape=(
-            jax.ShapeDtypeStruct((FIELDS * BLK_DEV, 128), f32),
+            jax.ShapeDtypeStruct((FIELDS, BLK_DEV, 128), f32),
             jax.ShapeDtypeStruct((BLK_DEV, 128), f32),
             jax.ShapeDtypeStruct((1, FOR_DEV), f32),
             jax.ShapeDtypeStruct((FIELDS, FOR_DEV), f32),
             jax.ShapeDtypeStruct((FIELDS, FOR_DEV), f32),
         ),
         in_specs=[vmem],
-        out_specs=(vmem,) * 5,
+        out_specs=(pl.BlockSpec(memory_space=pltpu.HBM),) + (vmem,) * 4,
         scratch_shapes=[
+            pltpu.VMEM((FIELDS, BLK_DEV, 128), f32),
             pltpu.VMEM((SLOTS + 8, 128), f32),
             pltpu.VMEM((2 * FIELDS + 8, FOR_DEV), f32),
             [pltpu.VMEM((CAP, 128), f32)] * 4,
             pltpu.VMEM((PEERS, 128), jnp.int32),
             [pltpu.SMEM((8, 128), jnp.int32)] * 2,
             pltpu.SemaphoreType.DMA((2,)),
+            pltpu.SemaphoreType.DMA((BLK_DEV // 8,)),
         ],
         compiler_params=pltpu.CompilerParams(vmem_limit_bytes=VMEM_LIMIT),
         name="place",
@@ -300,7 +313,7 @@
     outbox = pack(records, halo_mass, forest_id, dest_block, dest_slot)
     inbox = lax.all_to_all(outbox, EXCHANGE, split_axis=0, concat_axis=0, tiled=True)
     blocks, block_mass, fmass, fmean, fsecond = place(inbox)
-    return blocks.reshape(FIELDS, BLK_DEV, 128), block_mass, fmass.reshape(FOR_DEV), fmean, fsecond
+    return blocks, block_mass, fmass.reshape(FOR_DEV), fmean, fsecond
 
 
 def solution(mesh):

time: 72.9 us -> 67.7 us (0.929)
  local copies, waits for them, and re-layouts: 4.09 us -> 1.31 us
  Pallas kernels: 15.6 us -> 13.5 us
    unnamed x10, local copies, waits for them, and re-layouts: 4.09 us -> 1.31 us
    pallas_call x1, Pallas kernels: 6.38 us -> 4.5 us  [pack(): pl.pallas_call(pack_kernel, out_shape=jax.ShapeDtypeStruct((PEERS, ROWS,...]
    pallas_call x1 -> x2, Pallas kernels: 9.26 us -> 9.01 us  [the longest x1 8.39 us: place(): pl.pallas_call(place_kernel, out_shape=(jax.ShapeDtypeStruct((FIELDS, BLK...]
where the time goes in v3:
time: 67.7 us; the launch traced here: 67.5 us
  blocking collectives  52 us (77%)
  Pallas kernels  13.5 us (20%)
  local copies, waits for them, and re-layouts  1.31 us (2%)
    all_to_all x1, blocking collectives, on_device(): lax.all_to_all(outbox, EXCHANGE, split_axis=0, concat_axis=0, tiled=True)  52 us
    pallas_call x1, Pallas kernels, place(): pl.pallas_call(place_kernel, out_shape=(jax.ShapeDtypeStruct((FIELDS, BLK...  8.39 us
    pallas_call x1, Pallas kernels, pack(): pl.pallas_call(pack_kernel, out_shape=jax.ShapeDtypeStruct((PEERS, ROWS,...  4.5 us

profile of v3, /device:TPU:1, one launch (start us, length us, event | category | flops | bytes accessed | tf_op | source)
XLA Modules:
  0.0 67.5 jit_solution(1962127671616050570)
XLA Ops:
  0.6 0.0 copy-start.1
  0.6 0.7 %copy-done.1 = s32[4,1024]{1,0:T(4,128)S(1)} copy-done((s32[4,1024]{1,0:T(4,128)S(1)}, s32[4,1024]{1,0:T(4,128)}, u32[]{:S(2)}) %copy-start.1) | copy-done | bytes 16408
  1.4 0.0 copy-start
  1.4 0.0 copy-start.2
  1.4 0.0 copy-start.3
  1.4 0.0 copy-start.4
  1.4 0.6 rank.1
  2.0 0.6 copy-done
  2.6 0.0 copy-done.2
  2.6 0.0 copy-done.3
  2.6 0.0 copy-done.4
  2.6 4.5 %pack.1 = f32[64,48,128]{2,1,0:T(8,128)S(1)} custom-call(s32[32,128]{1,0:T(8,128)S(1)} %get-tuple-element.12.target_v, s32[32,128]{1,0:T(8,128)S(1)} %get-tuple-element.13.first_tag, f32[2048,128]{1,0:T(8,128)S(1)} %bitcast.26, f32[32,128]{1,0:T(8,128)S(1)} %bitcast.29, s32[32,128]{1,0:T(8,128)S(1)} %bitcast.30, s32[32,128]{1,0:T(8,128)S(1)} %bitcast.28, ...), custom_call_target="tpu_custom_call" | custom-call | tf_op jit(solution)/shard_map/pack/pallas_call | solution.py:266
  7.1 52.0 %all_to_all.5.msg = f32[64,48,128]{2,1,0:T(8,128)S(1)} all-to-all(f32[64,48,128]{2,1,0:T(8,128)S(1)} %pack.1), channel_id=1, replica_groups=mesh['row'=4,'sa'=4,'z2'=2,'z1'=2,'z0'=2,'core'=2] {'core','sa','z0','z1..., dimensions={0} | all-to-all | bytes 3145728 | tf_op jit(solution)/shard_map/all_to_all | solution.py:314
  59.1 8.4 %place.1 = (f32[64,40,128]{2,1,0:T(8,128)}, f32[40,128]{1,0:T(8,128)}, f32[1,128]{1,0:T(1,128)}, f32[64,128]{1,0:T(8,128)}, f32[64,128]{1,0:T(8,128)}) custom-call(f32[64,48,128]{2,1,0:T(8,128)S(1)} %all_to_all.5.msg), custom_call_target="tpu_custom_call" | custom-call | tf_op jit(solution)/shard_map/place/pallas_call | solution.py:286
Async XLA Ops:
  0.6 0.7 %copy-start.1 = (s32[4,1024]{1,0:T(4,128)S(1)}, s32[4,1024]{1,0:T(4,128)}, u32[]{:S(2)}) copy-start(s32[4,1024]{1,0:T(4,128)} %param.8) | copy-start | bytes 49156
  1.4 1.2 %copy-start = (f32[64,4,1024]{2,1,0:T(4,128)S(1)}, f32[64,4,1024]{2,1,0:T(4,128)}, u32[]{:S(2)}) copy-start(f32[64,4,1024]{2,1,0:T(4,128)} %param.5) | copy-start | bytes 3145732
  1.4 1.2 %copy-start.2 = (f32[4,1024]{1,0:T(4,128)S(1)}, f32[4,1024]{1,0:T(4,128)}, u32[]{:S(2)}) copy-start(f32[4,1024]{1,0:T(4,128)} %param.6) | copy-start | bytes 49156
  1.4 1.2 %copy-start.3 = (s32[4,1024]{1,0:T(4,128)S(1)}, s32[4,1024]{1,0:T(4,128)}, u32[]{:S(2)}) copy-start(s32[4,1024]{1,0:T(4,128)} %param.7) | copy-start | bytes 49156
  1.4 1.2 %copy-start.4 = (s32[4,1024]{1,0:T(4,128)S(1)}, s32[4,1024]{1,0:T(4,128)}, u32[]{:S(2)}) copy-start(s32[4,1024]{1,0:T(4,128)} %param.9) | copy-start | bytes 49156

commit v4 on v3

--- a/solution.py
+++ b/solution.py
@@ -14,6 +14,7 @@
 CAP = 88
 ROWS = 48
 TAGS = 48
+PITCH = 40
 VMEM_LIMIT = 24 * 1024 * 1024
 EXCHANGE = ("core", "sa", "z0", "z1", "z2")
 ROW_HA = ("row", "z2", "z1", "z0", "core")
@@ -35,17 +36,28 @@
     return core | plane | turned
 
 
-def rank_kernel(block, target, first_tag):
+def init_kernel(before, outbox, slots):
+    ordered = (iota((256, 384), 0) < iota((256, 384), 1)) | (iota((256, 384), 1) >= 256)
+    before[...] = ordered.astype(jnp.float32).astype(jnp.bfloat16)
+
+    for array in (outbox, slots):
+
+        def clear(k, carry):
+            array[pl.ds(pl.multiple_of(k * 128, 128), 128), :] = jnp.zeros((128, 128), jnp.float32)
+            return carry
+
+        lax.fori_loop(0, array.shape[0] // 128, clear, 0)
+
+
+def rank_kernel(block, before, target, first_tag):
     groups = block.shape[0]
-    before = (iota((256, 384), 0) < iota((256, 384), 1)) | (iota((256, 384), 1) >= 256)
-    before = before.astype(jnp.float32).astype(jnp.bfloat16)
     peer = iota((PEERS, 128), 0)
     base = jnp.zeros((PEERS, 128), jnp.float32)
     goal = position_of(owner_of(block[...]))
     for g in range(0, groups, 2):
         member = jnp.concatenate([peer == goal[g : g + 1], peer == goal[g + 1 : g + 2]], axis=1)
         counts = jnp.dot(
-            member.astype(jnp.float32).astype(jnp.bfloat16), before, preferred_element_type=jnp.float32
+            member.astype(jnp.float32).astype(jnp.bfloat16), before[...], preferred_element_type=jnp.float32
         )
         rank = counts[:, :256] + jnp.concatenate([base, base], axis=1)
         rank = jnp.sum(jnp.where(member, rank, 0.0), axis=0, keepdims=True).astype(jnp.int32)
@@ -58,8 +70,9 @@
 
 
 def pack_kernel(
-    target_v, first_tag, rec, mass, forest, block, slot_in, out, placed, slot, tiles, target_s, sems
+    target_v, first_tag, rec, mass, forest, block, slot_in, start, out, placed, slot, spaced, tiles, target_s, sems
 ):
+    del start
     groups = mass.shape[0]
 
     def index_copy(k, buf):
@@ -73,11 +86,8 @@
         tile[...] = jnp.zeros_like(tile)
     slot[...] = (block[...] - owner_of(block[...]) * BLK_DEV) * 128 + slot_in[...] + 1
 
-    def clear(k, carry):
-        placed[pl.ds(pl.multiple_of(k * 128, 128), 128), :] = jnp.zeros((128, 128), jnp.float32)
-        return carry
-
-    lax.fori_loop(0, PEERS * CAP // 128, clear, 0)
+    for f in range(FIELDS):
+        spaced[PITCH * f : PITCH * f + groups, :] = rec[groups * f : groups * f + groups, :]
     line = iota((TAGS, 128), 0)
 
     def turn(group, tile):
@@ -88,7 +98,7 @@
         tags = jnp.where(own_line == 0, row(mass), 0.0)
         tags = jnp.where(own_line == 1, row(slot).astype(jnp.float32), tags)
         tags = jnp.where(own_line == 2, (row(forest) & (FOR_DEV - 1)).astype(jnp.float32), tags)
-        stack = jnp.concatenate([rec[pl.ds(group, FIELDS, stride=groups), :], tags], axis=0)
+        stack = jnp.concatenate([spaced[pl.ds(group, FIELDS, stride=PITCH), :], tags], axis=0)
         tile[:, : FIELDS + TAGS] = stack.T
 
     turn(0, tiles[0])
@@ -103,14 +113,12 @@
             for r in range(128):
                 placed[pl.ds(target_s[i // 8][i % 8, r], 1), :] = tile[r : r + 1, :]
             if i % 8 == 7:
-
-                @pl.when(2 * k + i // 8 + 2 < groups // 8)
-                def _():
-                    index_copy(2 * k + i // 8 + 2, i // 8).start()
-
+                index_copy(jnp.minimum(2 * k + i // 8 + 2, groups // 8 - 1), i // 8).start()
         return carry
 
     lax.fori_loop(0, groups // 16, step, 0)
+    for buf in range(2):
+        index_copy(0, buf).wait()
 
     lane = iota((8, 128), 1)
     low = lane < FIELDS
@@ -134,9 +142,17 @@
 
 
 def place_kernel(
-    msg, blocks_hbm, block_mass, fmass, fmean, fsecond, blocks, placed, acc, tiles, slot_v, slot_s, sems, out_sems
+    msg, start, blocks_hbm, block_mass_hbm, fmass_hbm, fmean_hbm, fsecond_hbm, placed,
+    blocks, block_mass, fmass, fmean, fsecond, acc, tiles, slot_v, slot_s, sems, out_sems,
 ):
+    del start
     by_row = blocks.reshape(FIELDS * BLK_DEV, 128)
+
+    def index_copy(g, buf):
+        return pltpu.make_async_copy(
+            slot_v.at[pl.ds(pl.multiple_of(8 * g, 8), 8), :], slot_s[buf], sems.at[buf]
+        )
+
     lane = iota((8, 128), 1)
     low = lane < FIELDS
     slot_lane = (lane >= FIELDS) & (lane < FIELDS + 4 * (CAP // 8)) & (lane % 4 == 1)
@@ -151,20 +167,8 @@
             )
         index = index.astype(jnp.int32)
         slot_v[8 * g : 8 * g + 8, :] = jnp.where(index == 0, SLOTS, index - 1)
-
-    def index_copy(g, buf):
-        return pltpu.make_async_copy(
-            slot_v.at[pl.ds(pl.multiple_of(8 * g, 8), 8), :], slot_s[buf], sems.at[buf]
-        )
-
-    index_copy(0, 0).start()
-    index_copy(1, 1).start()
-
-    def clear(k, carry):
-        placed[pl.ds(pl.multiple_of(k * 128, 128), 128), :] = jnp.zeros((128, 128), jnp.float32)
-        return carry
-
-    lax.fori_loop(0, SLOTS // 128, clear, 0)
+        if g < 2:
+            index_copy(g, g).start()
     acc[...] = jnp.zeros_like(acc)
 
     def turn(p, tile):
@@ -189,14 +193,12 @@
                 col = r // 8 * 4 + i % 8 % 4 + i % 8 // 4 * 64
                 placed[pl.ds(slot_s[i // 8][r % 8, col], 1), :] = tile[r : r + 1, :]
             if i % 8 == 7:
-
-                @pl.when(2 * k + i // 8 + 2 < PEERS // 8)
-                def _():
-                    index_copy(2 * k + i // 8 + 2, i // 8).start()
-
+                index_copy(jnp.minimum(2 * k + i // 8 + 2, PEERS // 8 - 1), i // 8).start()
         return carry
 
     lax.fori_loop(0, PEERS // 16, step, 0)
+    for buf in range(2):
+        index_copy(0, buf).wait()
 
     owned = iota((FOR_DEV, 128), 0)
 
@@ -232,13 +234,23 @@
         return carry
 
     lax.fori_loop(0, BLK_DEV // 8, finish, 0)
+    others = [
+        pltpu.make_async_copy(src, dst, out_sems.at[BLK_DEV // 8 + n])
+        for n, (src, dst) in enumerate(
+            ((block_mass, block_mass_hbm), (fmass, fmass_hbm), (fmean, fmean_hbm), (fsecond, fsecond_hbm))
+        )
+    ]
+    others[0].start()
     weight = acc[2 * FIELDS : 2 * FIELDS + 1]
     mass_total = jnp.broadcast_to(total[0:1, 127:128], (1, FOR_DEV))
     fmass[...] = weight * (FOR_DEV * PEERS / mass_total)
+    others[1].start()
     fmean[...] = acc[:FIELDS] / weight
+    others[2].start()
     fsecond[...] = acc[FIELDS : 2 * FIELDS] / weight
-    for k in range(BLK_DEV // 8):
-        out_copy(k).wait()
+    others[3].start()
+    for copy in [out_copy(k) for k in range(BLK_DEV // 8)] + others:
+        copy.wait()
 
 
 def pack(records, halo_mass, forest_id, dest_block, dest_slot):
@@ -254,65 +266,77 @@
     row = (groups, 128)
     vmem = pl.BlockSpec(memory_space=pltpu.VMEM)
     params = pltpu.CompilerParams(vmem_limit_bytes=VMEM_LIMIT)
+    before, placed, slots = pl.pallas_call(
+        init_kernel,
+        out_shape=(
+            jax.ShapeDtypeStruct((256, 384), jnp.bfloat16),
+            jax.ShapeDtypeStruct((PEERS * CAP, 128), jnp.float32),
+            jax.ShapeDtypeStruct((SLOTS + 128, 128), jnp.float32),
+        ),
+        out_specs=(vmem,) * 3,
+        cost_estimate=pl.CostEstimate(flops=2**31, bytes_accessed=2**16, transcendentals=0),
+        compiler_params=params,
+        name="init",
+    )()
     target, first_tag = pl.pallas_call(
         rank_kernel,
         out_shape=(jax.ShapeDtypeStruct(row, jnp.int32),) * 2,
-        in_specs=[vmem],
+        in_specs=[vmem] * 2,
         out_specs=(vmem,) * 2,
-        cost_estimate=pl.CostEstimate(flops=2**31, bytes_accessed=2**16, transcendentals=0),
+        cost_estimate=pl.CostEstimate(flops=2**20, bytes_accessed=2**16, transcendentals=0),
         compiler_params=params,
         name="rank",
-    )(block)
-    return pl.pallas_call(
+    )(block, before)
+    outbox, _ = pl.pallas_call(
         pack_kernel,
-        out_shape=jax.ShapeDtypeStruct((PEERS, ROWS, 128), jnp.float32),
-        in_specs=[vmem] * 7,
-        out_specs=vmem,
+        out_shape=(
+            jax.ShapeDtypeStruct((PEERS, ROWS, 128), jnp.float32),
+            jax.ShapeDtypeStruct((PEERS * CAP, 128), jnp.float32),
+        ),
+        in_specs=[vmem] * 8,
+        out_specs=(vmem, pl.BlockSpec(memory_space=pltpu.VMEM)),
+        input_output_aliases={7: 1},
         scratch_shapes=[
-            pltpu.VMEM((PEERS * CAP, 128), jnp.float32),
             pltpu.VMEM(row, jnp.int32),
+            pltpu.VMEM((FIELDS * PITCH, 128), jnp.float32),
             [pltpu.VMEM((128, 128), jnp.float32)] * 4,
             [pltpu.SMEM((8, 128), jnp.int32)] * 2,
             pltpu.SemaphoreType.DMA((2,)),
         ],
         compiler_params=params,
         name="pack",
-    )(target, first_tag, records, mass, forest, block, slot)
-
-
-def place(msg):
+    )(target, first_tag, records, mass, forest, block, slot, placed)
+    return outbox, slots
+
+
+def place(msg, slots):
     f32 = jnp.float32
     vmem = pl.BlockSpec(memory_space=pltpu.VMEM)
+    shapes = ((FIELDS, BLK_DEV, 128), (BLK_DEV, 128), (1, FOR_DEV), (FIELDS, FOR_DEV), (FIELDS, FOR_DEV))
     return pl.pallas_call(
         place_kernel,
-        out_shape=(
-            jax.ShapeDtypeStruct((FIELDS, BLK_DEV, 128), f32),
-            jax.ShapeDtypeStruct((BLK_DEV, 128), f32),
-            jax.ShapeDtypeStruct((1, FOR_DEV), f32),
-            jax.ShapeDtypeStruct((FIELDS, FOR_DEV), f32),
-            jax.ShapeDtypeStruct((FIELDS, FOR_DEV), f32),
-        ),
-        in_specs=[vmem],
-        out_specs=(pl.BlockSpec(memory_space=pltpu.HBM),) + (vmem,) * 4,
-        scratch_shapes=[
-            pltpu.VMEM((FIELDS, BLK_DEV, 128), f32),
-            pltpu.VMEM((SLOTS + 8, 128), f32),
+        out_shape=tuple(jax.ShapeDtypeStruct(shape, f32) for shape in shapes + (slots.shape,)),
+        in_specs=[vmem] * 2,
+        out_specs=(pl.BlockSpec(memory_space=pltpu.HBM),) * 5 + (vmem,),
+        input_output_aliases={1: 5},
+        scratch_shapes=[pltpu.VMEM(shape, f32) for shape in shapes]
+        + [
             pltpu.VMEM((2 * FIELDS + 8, FOR_DEV), f32),
             [pltpu.VMEM((CAP, 128), f32)] * 4,
             pltpu.VMEM((PEERS, 128), jnp.int32),
             [pltpu.SMEM((8, 128), jnp.int32)] * 2,
             pltpu.SemaphoreType.DMA((2,)),
-            pltpu.SemaphoreType.DMA((BLK_DEV // 8,)),
+            pltpu.SemaphoreType.DMA((BLK_DEV // 8 + 4,)),
         ],
         compiler_params=pltpu.CompilerParams(vmem_limit_bytes=VMEM_LIMIT),
         name="place",
-    )(msg)
+    )(msg, slots)[:5]
 
 
 def on_device(records, halo_mass, forest_id, dest_block, dest_slot):
-    outbox = pack(records, halo_mass, forest_id, dest_block, dest_slot)
+    outbox, slots = pack(records, halo_mass, forest_id, dest_block, dest_slot)
     inbox = lax.all_to_all(outbox, EXCHANGE, split_axis=0, concat_axis=0, tiled=True)
-    blocks, block_mass, fmass, fmean, fsecond = place(inbox)
+    blocks, block_mass, fmass, fmean, fsecond = place(inbox, slots)
     return blocks, block_mass, fmass.reshape(FOR_DEV), fmean, fsecond
 
 

time: 67.7 us -> 67.1 us (level)
  local copies, waits for them, and re-layouts: 1.31 us -> 0.18 us
    unnamed x10, local copies, waits for them, and re-layouts: 1.31 us -> 0.18 us
    pallas_call x2 -> x3, Pallas kernels: 12.9 us -> 13.5 us  [the longest x1 8.38 us: place(): pl.pallas_call(place_kernel, out_shape=tuple((jax.ShapeDtypeStruct(shape,...]
where the time goes in v4:
time: 67.1 us; the launch traced here: 66.9 us
  blocking collectives  52 us (77%)
  Pallas kernels  14.1 us (21%)
  between operations  0.72 us (1%)
    all_to_all x1, blocking collectives, on_device(): lax.all_to_all(outbox, EXCHANGE, split_axis=0, concat_axis=0, tiled=True)  52 us
    pallas_call x1, Pallas kernels, place(): pl.pallas_call(place_kernel, out_shape=tuple((jax.ShapeDtypeStruct(shape,...  8.38 us
    pallas_call x1, Pallas kernels, pack(): pl.pallas_call(pack_kernel, out_shape=(jax.ShapeDtypeStruct((PEERS, ROWS,...  4.6 us

profile of v4, /device:TPU:1, one launch (start us, length us, event | category | flops | bytes accessed | tf_op | source)
XLA Modules:
  0.0 66.9 jit_solution(5740391221082707297)
XLA Ops:
  0.6 0.0 copy-start.1
  0.6 0.0 copy-start.4
  0.7 0.0 copy-start.3
  0.7 0.0 copy-start.2
  0.7 0.0 copy-start
  0.7 0.5 init.1
  1.2 0.2 copy-done.1
  1.4 0.6 rank.1
  1.9 0.0 copy-done.4
  1.9 0.0 copy-done.3
  1.9 0.0 copy-done.2
  2.0 0.0 copy-done
  2.0 4.6 %pack.1 = (f32[64,48,128]{2,1,0:T(8,128)S(1)}, f32[5632,128]{1,0:T(8,128)S(1)}) custom-call(s32[32,128]{1,0:T(8,128)S(1)} %get-tuple-element.17.target_v, s32[32,128]{1,0:T(8,128)S(1)} %get-tuple-element.18.first_tag, f32[2048,128]{1,0:T(8,128)S(1)} %bitcast.26, f32[32,128]{1,0:T(8,128)S(1)} %bitcast.29, ...), custom_call_target="tpu_custom_call", output_to_operand_aliasing={{1}: (7, {})} | custom-call | tf_op jit(solution)/shard_map/pack/pallas_call | solution.py:290
  6.6 52.0 %all_to_all.5.msg = f32[64,48,128]{2,1,0:T(8,128)S(1)} all-to-all(f32[64,48,128]{2,1,0:T(8,128)S(1)} %get-tuple-element.20), channel_id=1, replica_groups=mesh['row'=4,'sa'=4,'z2'=2,'z1'=2,'z0'=2,'core'=2] {'core','sa','z0','z1..., dimensions={0} | all-to-all | bytes 3145728 | tf_op jit(solution)/shard_map/all_to_all | solution.py:338
  58.6 8.4 %place.1 = (f32[64,40,128]{2,1,0:T(8,128)}, f32[40,128]{1,0:T(8,128)}, f32[1,128]{1,0:T(1,128)}, f32[64,128]{1,0:T(8,128)}, f32[64,128]{1,0:T(8,128)}, /*index=5*/f32[5248,128]{1,0:T(8,128)S(1)}) custom-call(f32[64,48,128]{2,1,0:T(8,128)S(1)} %all_to_all.5.msg, f32[5248,128]{1,0:T(8,128)S(1)} %get-tuple-element.21.start), custom_call_target="tpu_custom_call", output_to_operand_aliasing={{5}: (1, {})} | custom-call | tf_op jit(solution)/shard_map/place/pallas_call | solution.py:316
Async XLA Ops:
  0.6 0.7 %copy-start.1 = (s32[4,1024]{1,0:T(4,128)S(1)}, s32[4,1024]{1,0:T(4,128)}, u32[]{:S(2)}) copy-start(s32[4,1024]{1,0:T(4,128)} %param.8) | copy-start | bytes 49156
  0.6 1.3 %copy-start.4 = (s32[4,1024]{1,0:T(4,128)S(1)}, s32[4,1024]{1,0:T(4,128)}, u32[]{:S(2)}) copy-start(s32[4,1024]{1,0:T(4,128)} %param.9) | copy-start | bytes 49156
  0.7 1.3 %copy-start.3 = (s32[4,1024]{1,0:T(4,128)S(1)}, s32[4,1024]{1,0:T(4,128)}, u32[]{:S(2)}) copy-start(s32[4,1024]{1,0:T(4,128)} %param.7) | copy-start | bytes 49156
  0.7 1.3 %copy-start.2 = (f32[4,1024]{1,0:T(4,128)S(1)}, f32[4,1024]{1,0:T(4,128)}, u32[]{:S(2)}) copy-start(f32[4,1024]{1,0:T(4,128)} %param.6) | copy-start | bytes 49156
  0.7 1.3 %copy-start = (f32[64,4,1024]{2,1,0:T(4,128)S(1)}, f32[64,4,1024]{2,1,0:T(4,128)}, u32[]{:S(2)}) copy-start(f32[64,4,1024]{2,1,0:T(4,128)} %param.5) | copy-start | bytes 3145732

commit v5 on v4

--- a/solution.py
+++ b/solution.py
@@ -75,13 +75,11 @@
     del start
     groups = mass.shape[0]
 
-    def index_copy(k, buf):
-        return pltpu.make_async_copy(
-            target_v.at[pl.ds(pl.multiple_of(8 * k, 8), 8), :], target_s[buf], sems.at[buf]
-        )
-
-    index_copy(0, 0).start()
-    index_copy(1, 1).start()
+    def index_copy(k):
+        return pltpu.make_async_copy(target_v.at[8 * k : 8 * k + 8, :], target_s[k], sems.at[k])
+
+    for k in range(groups // 8):
+        index_copy(k).start()
     for tile in tiles:
         tile[...] = jnp.zeros_like(tile)
     slot[...] = (block[...] - owner_of(block[...]) * BLK_DEV) * 128 + slot_in[...] + 1
@@ -103,22 +101,14 @@
 
     turn(0, tiles[0])
 
-    def step(k, carry):
-        for i in range(16):
-            if i % 8 == 0:
-                index_copy(0, i // 8).wait()
-            after = jnp.minimum(16 * k + i + 1, groups - 1)
-            turn(after, tiles[(i + 1) % 4])
-            tile = tiles[i % 4]
-            for r in range(128):
-                placed[pl.ds(target_s[i // 8][i % 8, r], 1), :] = tile[r : r + 1, :]
-            if i % 8 == 7:
-                index_copy(jnp.minimum(2 * k + i // 8 + 2, groups // 8 - 1), i // 8).start()
-        return carry
-
-    lax.fori_loop(0, groups // 16, step, 0)
-    for buf in range(2):
-        index_copy(0, buf).wait()
+    for i in range(groups):
+        if i % 8 == 0:
+            index_copy(i // 8).wait()
+        if i + 1 < groups:
+            turn(i + 1, tiles[(i + 1) % 4])
+        tile = tiles[i % 4]
+        for r in range(128):
+            placed[pl.ds(target_s[i // 8][i % 8, r], 1), :] = tile[r : r + 1, :]
 
     lane = iota((8, 128), 1)
     low = lane < FIELDS
@@ -167,7 +157,7 @@
             )
         index = index.astype(jnp.int32)
         slot_v[8 * g : 8 * g + 8, :] = jnp.where(index == 0, SLOTS, index - 1)
-        if g < 2:
+        if g < 4:
             index_copy(g, g).start()
     acc[...] = jnp.zeros_like(acc)
 
@@ -184,20 +174,21 @@
     turn(0, tiles[0])
 
     def step(k, carry):
-        for i in range(16):
+        for i in range(32):
             if i % 8 == 0:
                 index_copy(0, i // 8).wait()
-            turn(jnp.minimum(16 * k + i + 1, PEERS - 1), tiles[(i + 1) % 4])
+            turn(jnp.minimum(32 * k + i + 1, PEERS - 1), tiles[(i + 1) % 4])
             tile = tiles[i % 4]
             for r in range(CAP):
                 col = r // 8 * 4 + i % 8 % 4 + i % 8 // 4 * 64
                 placed[pl.ds(slot_s[i // 8][r % 8, col], 1), :] = tile[r : r + 1, :]
             if i % 8 == 7:
-                index_copy(jnp.minimum(2 * k + i // 8 + 2, PEERS // 8 - 1), i // 8).start()
+                index_copy(jnp.minimum(4 * k + i // 8 + 4, PEERS // 8 - 1), i // 8).start()
+
         return carry
 
-    lax.fori_loop(0, PEERS // 16, step, 0)
-    for buf in range(2):
+    lax.fori_loop(0, PEERS // 32, step, 0)
+    for buf in range(4):
         index_copy(0, buf).wait()
 
     owned = iota((FOR_DEV, 128), 0)
@@ -300,8 +291,8 @@
             pltpu.VMEM(row, jnp.int32),
             pltpu.VMEM((FIELDS * PITCH, 128), jnp.float32),
             [pltpu.VMEM((128, 128), jnp.float32)] * 4,
-            [pltpu.SMEM((8, 128), jnp.int32)] * 2,
-            pltpu.SemaphoreType.DMA((2,)),
+            [pltpu.SMEM((8, 128), jnp.int32)] * (groups // 8),
+            pltpu.SemaphoreType.DMA((groups // 8,)),
         ],
         compiler_params=params,
         name="pack",
@@ -324,8 +315,8 @@
             pltpu.VMEM((2 * FIELDS + 8, FOR_DEV), f32),
             [pltpu.VMEM((CAP, 128), f32)] * 4,
             pltpu.VMEM((PEERS, 128), jnp.int32),
-            [pltpu.SMEM((8, 128), jnp.int32)] * 2,
-            pltpu.SemaphoreType.DMA((2,)),
+            [pltpu.SMEM((8, 128), jnp.int32)] * 4,
+            pltpu.SemaphoreType.DMA((4,)),
             pltpu.SemaphoreType.DMA((BLK_DEV // 8 + 4,)),
         ],
         compiler_params=pltpu.CompilerParams(vmem_limit_bytes=VMEM_LIMIT),

time: 67.1 us -> 66 us (0.984)
  Pallas kernels: 14.1 us -> 12.9 us
    pallas_call x1, Pallas kernels: 4.6 us -> 3.73 us  [pack(): pl.pallas_call(pack_kernel, out_shape=(jax.ShapeDtypeStruct((PEERS, ROWS,...]
where the time goes in v5:
time: 66 us; the launch traced here: 65.8 us
  blocking collectives  52 us (79%)
  Pallas kernels  12.9 us (20%)
  between operations  0.72 us (1%)
    all_to_all x1, blocking collectives, on_device(): lax.all_to_all(outbox, EXCHANGE, split_axis=0, concat_axis=0, tiled=True)  52 us
    pallas_call x1, Pallas kernels, place(): pl.pallas_call(place_kernel, out_shape=tuple((jax.ShapeDtypeStruct(shape,...  8.08 us
    pallas_call x1, Pallas kernels, pack(): pl.pallas_call(pack_kernel, out_shape=(jax.ShapeDtypeStruct((PEERS, ROWS,...  3.73 us

profile of v5, /device:TPU:1, one launch (start us, length us, event | category | flops | bytes accessed | tf_op | source)
XLA Modules:
  0.0 65.8 jit_solution(1184473756939147584)
XLA Ops:
  0.6 0.0 copy-start.1
  0.6 0.0 copy-start.4
  0.7 0.0 copy-start.3
  0.7 0.0 copy-start.2
  0.7 0.0 copy-start
  0.7 0.5 init.1
  1.2 0.2 copy-done.1
  1.4 0.6 rank.1
  1.9 0.0 copy-done.4
  1.9 0.0 copy-done.3
  1.9 0.0 copy-done.2
  2.0 0.0 copy-done
  2.0 3.7 %pack.1 = (f32[64,48,128]{2,1,0:T(8,128)S(1)}, f32[5632,128]{1,0:T(8,128)S(1)}) custom-call(s32[32,128]{1,0:T(8,128)S(1)} %get-tuple-element.17.target_v, s32[32,128]{1,0:T(8,128)S(1)} %get-tuple-element.18.first_tag, f32[2048,128]{1,0:T(8,128)S(1)} %bitcast.26, f32[32,128]{1,0:T(8,128)S(1)} %bitcast.29, ...), custom_call_target="tpu_custom_call", output_to_operand_aliasing={{1}: (7, {})} | custom-call | tf_op jit(solution)/shard_map/pack/pallas_call | solution.py:281
  5.7 52.0 %all_to_all.5.msg = f32[64,48,128]{2,1,0:T(8,128)S(1)} all-to-all(f32[64,48,128]{2,1,0:T(8,128)S(1)} %get-tuple-element.20), channel_id=1, replica_groups=mesh['row'=4,'sa'=4,'z2'=2,'z1'=2,'z0'=2,'core'=2] {'core','sa','z0','z1..., dimensions={0} | all-to-all | bytes 3145728 | tf_op jit(solution)/shard_map/all_to_all | solution.py:329
  57.7 8.1 %place.1 = (f32[64,40,128]{2,1,0:T(8,128)}, f32[40,128]{1,0:T(8,128)}, f32[1,128]{1,0:T(1,128)}, f32[64,128]{1,0:T(8,128)}, f32[64,128]{1,0:T(8,128)}, /*index=5*/f32[5248,128]{1,0:T(8,128)S(1)}) custom-call(f32[64,48,128]{2,1,0:T(8,128)S(1)} %all_to_all.5.msg, f32[5248,128]{1,0:T(8,128)S(1)} %get-tuple-element.21.start), custom_call_target="tpu_custom_call", output_to_operand_aliasing={{5}: (1, {})} | custom-call | tf_op jit(solution)/shard_map/place/pallas_call | solution.py:307
Async XLA Ops:
  0.6 0.7 %copy-start.1 = (s32[4,1024]{1,0:T(4,128)S(1)}, s32[4,1024]{1,0:T(4,128)}, u32[]{:S(2)}) copy-start(s32[4,1024]{1,0:T(4,128)} %param.8) | copy-start | bytes 49156
  0.6 1.3 %copy-start.4 = (s32[4,1024]{1,0:T(4,128)S(1)}, s32[4,1024]{1,0:T(4,128)}, u32[]{:S(2)}) copy-start(s32[4,1024]{1,0:T(4,128)} %param.9) | copy-start | bytes 49156
  0.7 1.3 %copy-start.3 = (s32[4,1024]{1,0:T(4,128)S(1)}, s32[4,1024]{1,0:T(4,128)}, u32[]{:S(2)}) copy-start(s32[4,1024]{1,0:T(4,128)} %param.7) | copy-start | bytes 49156
  0.7 1.3 %copy-start.2 = (f32[4,1024]{1,0:T(4,128)S(1)}, f32[4,1024]{1,0:T(4,128)}, u32[]{:S(2)}) copy-start(f32[4,1024]{1,0:T(4,128)} %param.6) | copy-start | bytes 49156
  0.7 1.3 %copy-start = (f32[64,4,1024]{2,1,0:T(4,128)S(1)}, f32[64,4,1024]{2,1,0:T(4,128)}, u32[]{:S(2)}) copy-start(f32[64,4,1024]{2,1,0:T(4,128)} %param.5) | copy-start | bytes 3145732

commit v6 on v5

--- a/solution.py
+++ b/solution.py
@@ -116,8 +116,8 @@
     corner = jnp.where(lane == 127, jnp.broadcast_to(total, (8, 128)), 0.0)
 
     def squeeze(k, carry):
-        for h in range(8):
-            p = 8 * k + h
+        for h in range(16):
+            p = 16 * k + h
             start = p * CAP
             rows = [placed[pl.ds(pl.multiple_of(start + 8 * v, 8), 8), :] for v in range(CAP // 8)]
             for v in range(5):
@@ -128,7 +128,7 @@
             out[p, 40:48, :] = jnp.where(low, rows[5], tags)
         return carry
 
-    lax.fori_loop(0, PEERS // 8, squeeze, 0)
+    lax.fori_loop(0, PEERS // 16, squeeze, 0)
 
 
 def place_kernel(
@@ -197,15 +197,15 @@
         part = pl.ds(8 * k if isinstance(k, int) else pl.multiple_of(8 * k, 8), 8)
         return pltpu.make_async_copy(blocks.at[:, part, :], blocks_hbm.at[:, part, :], out_sems.at[k])
 
-    def finish(k, carry):
+    def finish(k):
         highs, lows, members = [], [], []
         for h in range(8):
             b = 8 * k + h
-            view = placed[pl.ds(pl.multiple_of(b * 128, 128), 128), :].T
+            view = placed[b * 128 : b * 128 + 128, :].T
             x = view[:FIELDS]
             m = view[FIELDS : FIELDS + 1]
             by_row[pl.ds(b, FIELDS, stride=BLK_DEV), :] = x
-            block_mass[pl.ds(b, 1), :] = m
+            block_mass[b : b + 1, :] = m
             forest = view[FIELDS + 2 : FIELDS + 3].astype(jnp.int32)
             members.append((owned == forest).astype(jnp.float32).astype(jnp.bfloat16))
             scaled = m * x
@@ -222,9 +222,9 @@
                 (((1,), (1,)), ((), ())),
                 preferred_element_type=jnp.float32,
             )
-        return carry
-
-    lax.fori_loop(0, BLK_DEV // 8, finish, 0)
+
+    for k in range(BLK_DEV // 8):
+        finish(k)
     others = [
         pltpu.make_async_copy(src, dst, out_sems.at[BLK_DEV // 8 + n])
         for n, (src, dst) in enumerate(

time: 66 us -> 65 us (0.985)
  Pallas kernels: 12.9 us -> 11.9 us
    pallas_call x1, Pallas kernels: 8.08 us -> 7.34 us  [place(): pl.pallas_call(place_kernel, out_shape=tuple((jax.ShapeDtypeStruct(shape,...]
where the time goes in v6:
time: 65 us; the launch traced here: 64.8 us
  blocking collectives  52 us (80%)
  Pallas kernels  11.9 us (18%)
  between operations  0.72 us (1%)
    all_to_all x1, blocking collectives, on_device(): lax.all_to_all(outbox, EXCHANGE, split_axis=0, concat_axis=0, tiled=True)  52 us
    pallas_call x1, Pallas kernels, place(): pl.pallas_call(place_kernel, out_shape=tuple((jax.ShapeDtypeStruct(shape,...  7.34 us
    pallas_call x1, Pallas kernels, pack(): pl.pallas_call(pack_kernel, out_shape=(jax.ShapeDtypeStruct((PEERS, ROWS,...  3.46 us

profile of v6, /device:TPU:1, one launch (start us, length us, event | category | flops | bytes accessed | tf_op | source)
XLA Modules:
  0.0 64.8 jit_solution(7520007912117604833)
XLA Ops:
  0.6 0.0 copy-start.1
  0.6 0.0 copy-start.4
  0.7 0.0 copy-start.3
  0.7 0.0 copy-start.2
  0.7 0.0 copy-start
  0.7 0.5 init.1
  1.2 0.2 copy-done.1
  1.4 0.6 rank.1
  1.9 0.0 copy-done.4
  1.9 0.0 copy-done.3
  1.9 0.0 copy-done.2
  2.0 0.0 copy-done
  2.0 3.5 %pack.1 = (f32[64,48,128]{2,1,0:T(8,128)S(1)}, f32[5632,128]{1,0:T(8,128)S(1)}) custom-call(s32[32,128]{1,0:T(8,128)S(1)} %get-tuple-element.17.target_v, s32[32,128]{1,0:T(8,128)S(1)} %get-tuple-element.18.first_tag, f32[2048,128]{1,0:T(8,128)S(1)} %bitcast.26, f32[32,128]{1,0:T(8,128)S(1)} %bitcast.29, ...), custom_call_target="tpu_custom_call", output_to_operand_aliasing={{1}: (7, {})} | custom-call | tf_op jit(solution)/shard_map/pack/pallas_call | solution.py:281
  5.4 52.0 %all_to_all.5.msg = f32[64,48,128]{2,1,0:T(8,128)S(1)} all-to-all(f32[64,48,128]{2,1,0:T(8,128)S(1)} %get-tuple-element.20), channel_id=1, replica_groups=mesh['row'=4,'sa'=4,'z2'=2,'z1'=2,'z0'=2,'core'=2] {'core','sa','z0','z1..., dimensions={0} | all-to-all | bytes 3145728 | tf_op jit(solution)/shard_map/all_to_all | solution.py:329
  57.4 7.3 %place.1 = (f32[64,40,128]{2,1,0:T(8,128)}, f32[40,128]{1,0:T(8,128)}, f32[1,128]{1,0:T(1,128)}, f32[64,128]{1,0:T(8,128)}, f32[64,128]{1,0:T(8,128)}, /*index=5*/f32[5248,128]{1,0:T(8,128)S(1)}) custom-call(f32[64,48,128]{2,1,0:T(8,128)S(1)} %all_to_all.5.msg, f32[5248,128]{1,0:T(8,128)S(1)} %get-tuple-element.21.start), custom_call_target="tpu_custom_call", output_to_operand_aliasing={{5}: (1, {})} | custom-call | tf_op jit(solution)/shard_map/place/pallas_call | solution.py:307
Async XLA Ops:
  0.6 0.7 %copy-start.1 = (s32[4,1024]{1,0:T(4,128)S(1)}, s32[4,1024]{1,0:T(4,128)}, u32[]{:S(2)}) copy-start(s32[4,1024]{1,0:T(4,128)} %param.8) | copy-start | bytes 49156
  0.6 1.3 %copy-start.4 = (s32[4,1024]{1,0:T(4,128)S(1)}, s32[4,1024]{1,0:T(4,128)}, u32[]{:S(2)}) copy-start(s32[4,1024]{1,0:T(4,128)} %param.9) | copy-start | bytes 49156
  0.7 1.3 %copy-start.3 = (s32[4,1024]{1,0:T(4,128)S(1)}, s32[4,1024]{1,0:T(4,128)}, u32[]{:S(2)}) copy-start(s32[4,1024]{1,0:T(4,128)} %param.7) | copy-start | bytes 49156
  0.7 1.3 %copy-start.2 = (f32[4,1024]{1,0:T(4,128)S(1)}, f32[4,1024]{1,0:T(4,128)}, u32[]{:S(2)}) copy-start(f32[4,1024]{1,0:T(4,128)} %param.6) | copy-start | bytes 49156
  0.7 1.3 %copy-start = (f32[64,4,1024]{2,1,0:T(4,128)S(1)}, f32[64,4,1024]{2,1,0:T(4,128)}, u32[]{:S(2)}) copy-start(f32[64,4,1024]{2,1,0:T(4,128)} %param.5) | copy-start | bytes 3145732
